TPU v7x, 32 devices: a whole 2x2x4 slice. The times are simulated.
32 devices in a mesh: rep: 1, r: 8 (over y, z), s: 4 (over x, core).
Axes of the slice: x: 2, y: 2, z: 4, core: 2. Of those that a mesh axis runs over, the one named last changes fastest.
Arguments:
- x: bfloat16 [32, 4096, 512], P(('rep', 'r', 's'))
- dy: bfloat16 [32, 4096, 512], P(('rep', 'r', 's'))
- w_gate: bfloat16 [2, 512, 1408], P(None, 's')
- w_up: bfloat16 [2, 512, 1408], P(None, 's')
- w_down: bfloat16 [2, 1408, 512], P(None, 's')
- m_w_gate: float32 [2, 512, 1408], P(None, 's')
- m_w_up: float32 [2, 512, 1408], P(None, 's')
- m_w_down: float32 [2, 1408, 512], P(None, 's')
- v_w_gate: float32 [2, 512, 1408], P(None, 's')
- v_w_up: float32 [2, 512, 1408], P(None, 's')
- v_w_down: float32 [2, 1408, 512], P(None, 's')
Outputs:
- output 1: bfloat16 [2, 512, 1408], P('rep', 's')
- output 2: bfloat16 [2, 512, 1408], P('rep', 's')
- output 3: bfloat16 [2, 1408, 512], P('rep', 's')
- output 4: float32 [2, 512, 1408], P('rep', 's')
- output 5: float32 [2, 512, 1408], P('rep', 's')
- output 6: float32 [2, 1408, 512], P('rep', 's')
- output 7: float32 [2, 512, 1408], P('rep', 's')
- output 8: float32 [2, 512, 1408], P('rep', 's')
- output 9: float32 [2, 1408, 512], P('rep', 's')
All inputs are finite; a program needn't handle non-finite values.
Results may differ from a plain program's by a relative error of at most 0.022.
Values are sent between devices in bfloat16 or wider.
A program may use at most 2 GiB of HBM per device.

v0:
```python
import jax
import jax.numpy as jnp
from jax import lax
from jax.sharding import PartitionSpec as P

NAMES = ("w_gate", "w_up", "w_down")


def matmul(a, w):
    return jnp.dot(a, w, preferred_element_type=jnp.float32).astype(jnp.bfloat16)


def normed(h):
    wide = h.astype(jnp.float32)
    scale = lax.rsqrt(jnp.mean(wide**2, -1, keepdims=True) + 1e-6)
    return (wide * scale).astype(jnp.bfloat16)


def layer(h, w):
    a = normed(h)
    gate = jnp.dot(a, w["w_gate"], preferred_element_type=jnp.float32)
    up = jnp.dot(a, w["w_up"], preferred_element_type=jnp.float32)
    return h + matmul((jax.nn.silu(gate) * up).astype(jnp.bfloat16), w["w_down"])


def adamw(w, m, v, g):
    m = 0.9 * m + 0.1 * g
    v = 0.95 * v + 0.05 * g * g
    step = m * lax.rsqrt(v + 1e-8) + 0.1 * w
    return (w - 0.02 * step).astype(jnp.bfloat16), m, v


def clipped(gradients, sum_of_squares, count):
    factor = jnp.minimum(1.0, 0.5 * lax.rsqrt(sum_of_squares / count + 1e-30))
    return [g * factor for g in gradients]


def solution(mesh):
    def fetched(weights, number):
        return {name: lax.all_gather(w[number], "s", axis=0, tiled=True) for name, w in zip(NAMES, weights, strict=True)}

    def summed(term):
        return lax.psum(lax.psum_scatter(term, "s", scatter_dimension=0, tiled=True), "r")

    def step(x, dy, *arrays):
        weights, m, v = (arrays[i : i + 3] for i in (0, 3, 6))
        layers = weights[0].shape[0]
        h, kept = x[0], []
        for number in range(layers):
            kept.append(h)
            h = layer(h, fetched(weights, number))
        by_h, mine = dy[0], [None] * layers
        for number in reversed(range(layers)):
            _, back = jax.vjp(lambda w, h: layer(h, w), fetched(weights, number), kept[number])
            by_w, by_h = back(by_h)
            mine[number] = [summed(by_w[name]) for name in NAMES]
        gradients = [jnp.stack([mine[number][i] for number in range(layers)]).astype(jnp.float32) for i in range(3)]
        squares = lax.psum(sum(jnp.sum(g * g) for g in gradients), "s")
        gradients = clipped(gradients, squares, lax.psum(1, "s") * sum(g.size for g in gradients))
        new = [adamw(w.astype(jnp.float32), m, v, g) for w, m, v, g in zip(weights, m, v, gradients, strict=True)]
        return tuple(one[which] for which in range(3) for one in new)

    states, cut = P(("rep", "r", "s"), None, None), P(None, "s", None)
    return jax.shard_map(
        step,
        mesh=mesh,
        in_specs=(states, states) + (cut,) * 9,
        out_specs=(P("rep", "s", None),) * 9,
        check_vma=False,
    )
```

profile of v0, /device:TPU:0, one launch (start us, length us, event | category | flops | bytes accessed | tf_op | source)
XLA Modules:
  0.0 532.7 jit_solution(1637014509341259684)
XLA Ops:
  15.2 6.4 %copy.20 = bf16[1,4096,512]{1,2,0:T(8,128)(2,1)} copy(bf16[1,4096,512]{2,1,0:T(8,128)(2,1)} %param.11) | data formatting | bytes 8388608 | tf_op args[0]
  31.6 13.2 %fusion.47 = f32[4096,1408]{1,0:T(8,128)} fusion(bf16[1,4096,512]{1,2,0:T(8,128)(2,1)} %copy.20, f32[4096]{0:T(1024)S(1)} %add_rsqrt_fusion, bf16[1,512,1408]{2,1,0:T(8,128)(2,1)} %all-gather.13.cloned.1.call-done), kind=kOutput, calls=%fused_computation.57 | convolution fusion | flops 5911871488 | bytes 28721152 | tf_op jit(solution)/shard_map/dot_general | solution.py:21
  44.8 7.7 %all-gather.15.cloned.1.call-done = bf16[1,512,1408]{2,1,0:T(8,128)(2,1)} async-done(((bf16[1,128,1408]{2,1,0:T(8,128)(2,1)}), bf16[1,512,1408]{2,1,0:T(8,128)(2,1)}) %all-gather.15.cloned.1.call-update) | async-done | bytes 1441808 | tf_op jit(solution)/shard_map/all_gather | solution.py:40
  52.4 24.3 %multiply_convert_fusion.1 = (bf16[4096,1408]{1,0:T(8,128)(2,1)}, f32[4096,1408]{1,0:T(8,128)}) fusion(f32[4096,1408]{1,0:T(8,128)} %fusion.47, bf16[1,512,1408]{2,1,0:T(8,128)(2,1)} %all-gather.15.cloned.1.call-done, bf16[1,4096,512]{1,2,0:T(8,128)(2,1)} %copy.20, f32[4096]{0:T(1024)S(1)} %add_rsqrt_fusion), kind=kOutput, calls=%fused_computation.17 | convolution fusion | flops 5946474496 | bytes 63324160 | tf_op jit(solution)/shard_map/dot_general | solution.py:22
  76.8 12.5 %fusion.19 = (f32[4096]{0:T(1024)S(1)}, bf16[4096,512]{0,1:T(8,128)(2,1)}) fusion(bf16[4096,1408]{1,0:T(8,128)(2,1)} %get-tuple-element.30, bf16[1,1408,512]{2,1,0:T(8,128)(2,1)} %all-gather.17.cloned.1.call-done, bf16[1,4096,512]{1,2,0:T(8,128)(2,1)} %copy.20), kind=kOutput, calls=%fused_computation.37 | convolution fusion | flops 5916061696 | bytes 21381120 | tf_op jit(solution)/shard_map/dot_general | solution.py:10
  94.0 11.9 %convolution_convert_fusion.1 = bf16[4096,1408]{1,0:T(8,128)(2,1)} fusion(bf16[1,4096,512]{2,1,0:T(8,128)(2,1)} %param.12, bf16[1,1408,512]{2,1,0:T(8,128)(2,1)} %all-gather.21.cloned.1.call-done), kind=kOutput, calls=%fused_computation.23 | convolution fusion | flops 5911347200 | bytes 17170432 | tf_op jit(solution)/shard_map/transpose(jvp())/dot_general | solution.py:10
  105.9 8.8 %all-gather.23.cloned.1.call-done = bf16[1,512,1408]{2,1,0:T(8,128)(2,1)} async-done(((bf16[1,128,1408]{2,1,0:T(8,128)(2,1)}), bf16[1,512,1408]{2,1,0:T(8,128)(2,1)}) %all-gather.23.cloned.1.call-update) | async-done | bytes 1441808 | tf_op jit(solution)/shard_map/all_gather | solution.py:40
  114.7 13.1 %fusion.39 = f32[4096,1408]{1,0:T(8,128)} fusion(bf16[4096,512]{0,1:T(8,128)(2,1)} %get-tuple-element.33, f32[4096]{0:T(1024)S(1)} %fusion.79, bf16[1,512,1408]{2,1,0:T(8,128)(2,1)} %all-gather.23.cloned.1.call-done), kind=kOutput, calls=%fused_computation.54 | convolution fusion | flops 5911871488 | bytes 28721152 | tf_op jit(solution)/shard_map/jvp()/dot_general | solution.py:22
  127.8 7.6 %all-gather.19.cloned.1.call-done = bf16[1,512,1408]{2,1,0:T(8,128)(2,1)} async-done(((bf16[1,128,1408]{2,1,0:T(8,128)(2,1)}), bf16[1,512,1408]{2,1,0:T(8,128)(2,1)}) %all-gather.19.cloned.1.call-update) | async-done | bytes 1441808 | tf_op jit(solution)/shard_map/all_gather | solution.py:40
  135.4 31.7 %fusion.2 = (bf16[4096,1408]{1,0:T(8,128)(2,1)}, f32[4096,1408]{1,0:T(8,128)}) fusion(f32[4096,1408]{1,0:T(8,128)} %fusion.39, bf16[4096,1408]{1,0:T(8,128)(2,1)} %convolution_convert_fusion.1, bf16[1,512,1408]{2,1,0:T(8,128)(2,1)} %all-gather.19.cloned.1.call-done, bf16[4096,512]{0,1:T(8,128)(2,1)} %get-tuple-element.33, f32[4096]{0:T(1024)S(1)} %fusion.79), kind=kOutput, calls=%fused_computation.8 | convolution fusion | flops 5981077504 | bytes 74858496 | tf_op jit(solution)/shard_map/jvp()/dot_general | solution.py:21
  167.2 12.8 %convolution_convert_fusion.5 = bf16[512,1408]{1,0:T(8,128)(2,1)} fusion(bf16[4096,1408]{1,0:T(8,128)(2,1)} %get-tuple-element.34, bf16[4096,512]{0,1:T(8,128)(2,1)} %get-tuple-element.33, f32[4096]{0:T(1024)S(1)} %fusion.79), kind=kOutput, calls=%fused_computation.53 | convolution fusion | flops 5911871488 | bytes 17186816 | tf_op jit(solution)/shard_map/transpose(jvp())/dot_general | solution.py:21
  180.0 17.2 %fusion.22 = bf16[4096,512]{0,1:T(8,128)(2,1)} fusion(bf16[4096,1408]{1,0:T(8,128)(2,1)} %convolution_convert_fusion.1, bf16[1,512,1408]{2,1,0:T(8,128)(2,1)} %all-gather.23.cloned.1.call-done, f32[4096,1408]{1,0:T(8,128)} %get-tuple-element.35), kind=kOutput, calls=%fused_computation.40 | convolution fusion | flops 5942280192 | bytes 40239104 | tf_op jit(solution)/shard_map/transpose(jvp())/dot_general | solution.py:22
  197.2 11.1 %fusion.21 = (f32[4096]{0:T(1024)S(1)}, bf16[4096,512]{0,1:T(8,128)(2,1)S(1)}) fusion(bf16[4096,512]{0,1:T(8,128)(2,1)S(1)} %copy-done.1, bf16[4096,512]{0,1:T(8,128)(2,1)} %fusion.22, bf16[4096,1408]{1,0:T(8,128)(2,1)} %get-tuple-element.34, bf16[1,512,1408]{2,1,0:T(8,128)(2,1)} %all-gather.19.cloned.1.call-done), kind=kOutput, calls=%fused_computation.39 | convolution fusion | flops 5916061696 | bytes 25575424 | tf_op jit(solution)/shard_map/transpose(jvp())/dot_general | solution.py:21
  211.3 9.6 %convolution_convert_fusion = bf16[4096,1408]{1,0:T(8,128)(2,1)} fusion(bf16[4096,512]{0,1:T(8,128)(2,1)S(1)} %fusion.25, bf16[1,1408,512]{2,1,0:T(8,128)(2,1)S(1)} %copy-done.18), kind=kOutput, calls=%fused_computation.22 | convolution fusion | flops 5911347200 | bytes 17170432 | tf_op jit(solution)/shard_map/transpose(jvp())/dot_general | solution.py:10
  220.9 24.5 %fusion.33 = bf16[512,1408]{1,0:T(8,128)(2,1)} fusion(f32[4096,1408]{1,0:T(8,128)} %fusion.47, f32[4096,1408]{1,0:T(8,128)} %get-tuple-element.31, bf16[4096,1408]{1,0:T(8,128)(2,1)} %convolution_convert_fusion, bf16[1,4096,512]{1,2,0:T(8,128)(2,1)} %copy.20, f32[4096]{0:T(1024)S(1)} %copy-done.17), kind=kOutput, calls=%fused_computation.50 | convolution fusion | flops 5976031232 | bytes 63324160 | tf_op jit(solution)/shard_map/transpose(jvp())/dot_general | solution.py:21
  245.5 17.2 %fusion.32 = bf16[512,1408]{1,0:T(8,128)(2,1)} fusion(bf16[4096,1408]{1,0:T(8,128)(2,1)} %convolution_convert_fusion.1, bf16[4096,512]{0,1:T(8,128)(2,1)} %get-tuple-element.33, f32[4096]{0:T(1024)S(1)} %fusion.79, f32[4096,1408]{1,0:T(8,128)} %get-tuple-element.35), kind=kOutput, calls=%fused_computation.49 | convolution fusion | flops 5947195392 | bytes 40255488 | tf_op jit(solution)/shard_map/transpose(jvp())/dot_general | solution.py:22
  262.8 17.6 %fusion.36 = bf16[512,1408]{1,0:T(8,128)(2,1)} fusion(bf16[4096,1408]{1,0:T(8,128)(2,1)} %convolution_convert_fusion, f32[4096,1408]{1,0:T(8,128)} %fusion.47, bf16[1,4096,512]{1,2,0:T(8,128)(2,1)} %copy.20, f32[4096]{0:T(1024)S(1)} %copy-done.17), kind=kOutput, calls=%fused_computation.51 | convolution fusion | flops 5947195392 | bytes 40255488 | tf_op jit(solution)/shard_map/transpose(jvp())/dot_general | solution.py:22
  280.5 20.4 %fusion.29 = bf16[1408,512]{1,0:T(8,128)(2,1)} fusion(bf16[1,4096,512]{2,1,0:T(8,128)(2,1)} %param.12, f32[4096,1408]{1,0:T(8,128)} %fusion.39, f32[4096,1408]{1,0:T(8,128)} %get-tuple-element.35), kind=kOutput, calls=%fused_computation.48 | convolution fusion | flops 5940903936 | bytes 51773440 | tf_op jit(solution)/shard_map/transpose(jvp())/dot_general | solution.py:10
  300.9 12.2 %convolution_convert_fusion.4 = bf16[1408,512]{1,0:T(8,128)(2,1)} fusion(bf16[4096,1408]{1,0:T(8,128)(2,1)} %get-tuple-element.30, bf16[4096,512]{0,1:T(8,128)(2,1)} %copy-done.2), kind=kOutput, calls=%fused_computation.52 | convolution fusion | flops 5906300928 | bytes 17170432 | tf_op jit(solution)/shard_map/transpose(jvp())/dot_general | solution.py:10
  313.5 19.6 %reduce-scatter.11.cloned.1.call-done = bf16[128,1408]{1,0:T(8,128)(2,1)} async-done(((bf16[512,1408]{1,0:T(8,128)(2,1)}), bf16[128,1408]{1,0:T(8,128)(2,1)}) %reduce-scatter.11.cloned.1.call-update) | async-done | bytes 360464 | tf_op jit(solution)/shard_map/reduce_scatter | solution.py:43
  333.0 30.3 %reduce-scatter.17.cloned.1.call-done = bf16[352,512]{1,0:T(8,128)(2,1)} async-done(((bf16[1408,512]{1,0:T(8,128)(2,1)}), bf16[352,512]{1,0:T(8,128)(2,1)}) %reduce-scatter.17.cloned.1.call-update) | async-done | bytes 360464 | tf_op jit(solution)/shard_map/reduce_scatter | solution.py:43
  363.3 30.1 %reduce-scatter.15.cloned.1.call-done = bf16[352,512]{1,0:T(8,128)(2,1)} async-done(((bf16[1408,512]{1,0:T(8,128)(2,1)}), bf16[352,512]{1,0:T(8,128)(2,1)}) %reduce-scatter.15.cloned.1.call-update) | async-done | bytes 360464 | tf_op jit(solution)/shard_map/reduce_scatter | solution.py:43
  393.5 108.3 %all-reduce.3.cloned.1.call-done = (bf16[1,128,1408]{2,1,0:T(8,128)(2,1)}, bf16[1,128,1408]{2,1,0:T(8,128)(2,1)}, bf16[1,128,1408]{2,1,0:T(8,128)(2,1)}, bf16[1,...) async-done(((bf16[1,128,1408]{2,1,0:T(8,128)(2,1)}, bf16[1,128,1408]{2,1,0:T(8,128)(2,1)}, bf16[1,128,1408]{2,1,0:T(8,128)(2,1)}, ...) | async-done | bytes 2162704 | tf_op jit(solution)/shard_map/psum | solution.py:43
  510.1 6.8 %psum.55 = f32[]{:T(128)} all-reduce(f32[]{:T(128)S(6)} %add.111), channel_id=1, replica_groups=mesh['rep'=1,'r'=8,'s'=4] {'s'}, use_global_device_ids=true, to_apply=%region_18.19 | all-reduce | flops 1 | bytes 8 | tf_op jit(solution)/shard_map/psum | solution.py:58
  (84 shorter events, 40.9 us)
Async XLA Ops:
  7.2 24.4 %all-gather.13.cloned.1.call-start = ((), (), s32[]{:S(2)}) async-start(), calls=%async_computation.12 | async-start | bytes 1802240 | tf_op jit(solution)/shard_map/all_gather | solution.py:40
  9.2 43.2 %all-gather.15.cloned.1.call-start = ((), (), s32[]{:S(2)}) async-start(), calls=%async_computation.13 | async-start | bytes 1802240 | tf_op jit(solution)/shard_map/all_gather | solution.py:40
  11.3 65.4 %all-gather.17.cloned.1.call-start = ((), (), s32[]{:S(2)}) async-start(), calls=%async_computation.14 | async-start | bytes 1802240 | tf_op jit(solution)/shard_map/all_gather | solution.py:40
  13.4 80.6 %all-gather.21.cloned.1.call-start = ((), (), s32[]{:S(2)}) async-start(), calls=%async_computation.16 | async-start | bytes 1802240 | tf_op jit(solution)/shard_map/all_gather | solution.py:40
  14.0 100.7 %all-gather.23.cloned.1.call-start = ((), (), s32[]{:S(2)}) async-start(), calls=%async_computation.17 | async-start | bytes 1802240 | tf_op jit(solution)/shard_map/all_gather | solution.py:40
  14.6 120.8 %all-gather.19.cloned.1.call-start = ((), (), s32[]{:S(2)}) async-start(), calls=%async_computation.15 | async-start | bytes 1802240 | tf_op jit(solution)/shard_map/all_gather | solution.py:40
  15.1 298.3 %reduce-scatter.9.cloned.1.call-start = ((), (), s32[]{:S(2)}) async-start(), calls=%async_computation.7 | async-start | bytes 1802240 | tf_op jit(solution)/shard_map/reduce_scatter | solution.py:43
  24.6 27.8 %copy-start.16 = (f32[4096]{0:T(1024)}, f32[4096]{0:T(1024)S(1)}, u32[]{:S(2)}) copy-start(f32[4096]{0:T(1024)S(1)} %add_rsqrt_fusion) | copy-start | bytes 49156
  89.2 16.7 %copy-start.14 = (f32[4096]{0:T(1024)}, f32[4096]{0:T(1024)S(1)}, u32[]{:S(2)}) copy-start(f32[4096]{0:T(1024)S(1)} %get-tuple-element.32) | copy-start | bytes 49156
  180.0 133.5 %reduce-scatter.7.cloned.1.call-start = ((), (), s32[]{:S(2)}) async-start(), calls=%async_computation.6 | async-start | bytes 1802240 | tf_op jit(solution)/shard_map/reduce_scatter | solution.py:43
  180.0 17.2 %copy-start.1 = (bf16[4096,512]{0,1:T(8,128)(2,1)S(1)}, bf16[4096,512]{0,1:T(8,128)(2,1)}, u32[]{:S(2)}) copy-start(bf16[4096,512]{0,1:T(8,128)(2,1)} %get-tuple-element.33) | copy-start | bytes 12582916
  197.2 11.2 %copy-start.15 = (f32[4096]{0:T(1024)S(1)}, f32[4096]{0:T(1024)}, u32[]{:S(2)}) copy-start(f32[4096]{0:T(1024)} %copy-done.14) | copy-start | bytes 49156
  197.2 11.2 %copy-start = (bf16[1,4096,512]{1,2,0:T(8,128)(2,1)S(1)}, bf16[1,4096,512]{1,2,0:T(8,128)(2,1)}, u32[]{:S(2)}) copy-start(bf16[1,4096,512]{1,2,0:T(8,128)(2,1)} %copy.21) | copy-start | bytes 12582916
  245.5 68.0 %reduce-scatter.13.cloned.1.call-start = ((), (), s32[]{:S(2)}) async-start(), calls=%async_computation.9 | async-start | bytes 1802240 | tf_op jit(solution)/shard_map/reduce_scatter | solution.py:43
  262.7 70.3 %reduce-scatter.11.cloned.1.call-start = ((), (), s32[]{:S(2)}) async-start(), calls=%async_computation.8 | async-start | bytes 1802240 | tf_op jit(solution)/shard_map/reduce_scatter | solution.py:43
  280.4 82.9 %reduce-scatter.17.cloned.1.call-start = ((), (), s32[]{:S(2)}) async-start(), calls=%async_computation.11 | async-start | bytes 1802240 | tf_op jit(solution)/shard_map/reduce_scatter | solution.py:43
  300.9 92.6 %reduce-scatter.15.cloned.1.call-start = ((), (), s32[]{:S(2)}) async-start(), calls=%async_computation.10 | async-start | bytes 1802240 | tf_op jit(solution)/shard_map/reduce_scatter | solution.py:43
  313.1 204.5 %copy-start.5 = (bf16[2,352,512]{2,1,0:T(8,128)(2,1)S(1)}, bf16[2,352,512]{2,1,0:T(8,128)(2,1)}, u32[]{:S(2)}) copy-start(bf16[2,352,512]{2,1,0:T(8,128)(2,1)} %param.15) | copy-start | bytes 2162692
  313.2 188.6 %all-reduce.3.cloned.1.call-start = ((), (), s32[]{:S(2)}) async-start(), calls=%async_computation.18 | async-start | bytes 4325376 | tf_op jit(solution)/shard_map/psum | solution.py:43
  507.2 15.0 %copy-start.3 = (bf16[2,128,1408]{2,1,0:T(8,128)(2,1)S(1)}, bf16[2,128,1408]{2,1,0:T(8,128)(2,1)}, u32[]{:S(2)}) copy-start(bf16[2,128,1408]{2,1,0:T(8,128)(2,1)} %param.13) | copy-start | bytes 2162692
  507.2 14.9 %copy-start.4 = (bf16[2,128,1408]{2,1,0:T(8,128)(2,1)S(1)}, bf16[2,128,1408]{2,1,0:T(8,128)(2,1)}, u32[]{:S(2)}) copy-start(bf16[2,128,1408]{2,1,0:T(8,128)(2,1)} %param.14) | copy-start | bytes 2162692
  507.2 14.9 %copy-start.10 = (bf16[1,128,1408]{2,1,0:T(8,128)(2,1)S(1)}, bf16[1,128,1408]{2,1,0:T(8,128)(2,1)}, u32[]{:S(2)}) copy-start(bf16[1,128,1408]{2,1,0:T(8,128)(2,1)} %get-tuple-element.9) | copy-start | bytes 1081348
  507.2 14.9 %copy-start.11 = (bf16[1,128,1408]{2,1,0:T(8,128)(2,1)S(1)}, bf16[1,128,1408]{2,1,0:T(8,128)(2,1)}, u32[]{:S(2)}) copy-start(bf16[1,128,1408]{2,1,0:T(8,128)(2,1)} %get-tuple-element.10) | copy-start | bytes 1081348
  507.2 14.9 %copy-start.12 = (bf16[1,128,1408]{2,1,0:T(8,128)(2,1)S(1)}, bf16[1,128,1408]{2,1,0:T(8,128)(2,1)}, u32[]{:S(2)}) copy-start(bf16[1,128,1408]{2,1,0:T(8,128)(2,1)} %get-tuple-element.11) | copy-start | bytes 1081348
  (8 other events, 44.7 us)
Sparse Core Ops, SparseCore 0:
  10.1 21.4 all-gather.12
  33.7 18.6 all-gather.14
  54.6 18.6 all-gather.16
  75.3 18.6 all-gather.20
  96.0 18.6 all-gather.22
  116.7 18.6 all-gather.18
  180.1 27.0 reduce-scatter.8
  245.6 27.0 reduce-scatter.6
  275.8 27.0 reduce-scatter.12
  305.9 27.0 reduce-scatter.10
  336.2 27.0 reduce-scatter.16
  366.3 27.0 reduce-scatter.14
  397.8 103.9 all-reduce.2
where the time goes:
time: 542 us; the launch traced here: 533 us
  matrix products  249 us (46%)
  waiting for transfers between devices  219 us (40%)
  other arithmetic  20.6 us (4%)
  local copies, waits for them, and re-layouts  18.8 us (3%)
  between operations  17 us (3%)
  blocking collectives  6.83 us (1%)
    psum x1, waiting for transfers between devices, summed(): lax.psum(lax.psum_scatter(term, 's', scatter_dimension=0, tiled=True), 'r')  108 us
    dot_general x5, matrix products, layer(): gate = jnp.dot(a, w['w_gate'], preferred_element_type=jnp.float32)  93.4 us
    dot_general x5, matrix products, layer(): up = jnp.dot(a, w['w_up'], preferred_element_type=jnp.float32)  89.4 us
    reduce_scatter x6, waiting for transfers between devices, summed(): lax.psum_scatter(term, 's', scatter_dimension=0, tiled=True)  80 us
    dot_general x5, matrix products, matmul(): jnp.dot(a, w, preferred_element_type=jnp.float32).astype(jnp.bfloat16)  66.6 us
    all_gather x6, waiting for transfers between devices, fetched(): lax.all_gather(w[number], 's', axis=0, tiled=True)  29.4 us
    unnamed x40, local copies, waits for them, and re-layouts  12.8 us
  transfers between devices with their start and end apart: 13, of which 9 were waited for; matrix products, arithmetic and copies ran while one was open for 43% of the time, Pallas kernels for 0%

commit v1 on v0

v1 whole, which is shorter than its diff:
```python
import functools

import jax
import jax.numpy as jnp
from jax import lax
from jax.experimental import pallas as pl
from jax.experimental.pallas import tpu as pltpu
from jax.sharding import PartitionSpec as P

F32, BF = jnp.float32, jnp.bfloat16
D, FF, TT = 512, 1408, 512
UNITS, SEG = 11, 32
ALL = 2 * UNITS
CHUNKS = ((0, 3), (3, 3), (6, 3), (9, 2))
COUNT = 2 * 3 * D * FF
VMEM_LIMIT = 62 * 2**20


def nn(a, b):
    return lax.dot_general(a, b, (((1,), (0,)), ((), ())), preferred_element_type=F32)


def nt(a, b):
    return lax.dot_general(a, b, (((1,), (1,)), ((), ())), preferred_element_type=F32)


def sigmoid(g):
    return 0.5 * jnp.tanh(0.5 * g) + 0.5


def backward_unit(g, u, d):
    s = sigmoid(g)
    silu = g * s
    return (silu * u).astype(BF), (d * u * (s + silu * (1.0 - s))).astype(BF), (d * silu).astype(BF)


def place():
    r, s = lax.axis_index("r"), lax.axis_index("s")
    return s // 2, s % 2, r // 4, r % 4


def device(x, core, y, z):
    return (0, y * 4 + z, x * 2 + core)


def remote(src, dst, send, recv, where):
    return pltpu.make_async_remote_copy(
        src_ref=src, dst_ref=dst, send_sem=send, recv_sem=recv, device_id=where, device_id_type=pl.DeviceIdType.MESH
    )


def greet(peers):
    barrier = pltpu.get_barrier_semaphore()
    for peer in peers:
        pl.semaphore_signal(barrier, inc=1, device_id=peer, device_id_type=pl.DeviceIdType.MESH)
    return lambda: pl.semaphore_wait(barrier, len(peers))


def pack(n, acc_gu, acc_d, row, out):
    for core in range(2):
        for x in range(2):
            s = 2 * x + core
            for p in range(8):
                y, z = p // 4, p % 4
                gu = pl.ds(pl.multiple_of(256 * row + 32 * p, 32), 32)
                d = pl.ds(pl.multiple_of(128 * row + SEG * s + 16 * y, 16), 16)
                out[n, core, x, p, 0:32, :] = acc_gu[gu, 128 * s : 128 * s + 128].astype(BF)
                out[n, core, x, p, 32:48, :] = acc_d[d, 128 * z : 128 * z + 128].astype(BF)


def first_kernel(
    x_ref, dy_ref, gate_ref, up_ref, down_ref, u_ref, dh_ref, wgu_out, wd_out,
    wgu, wd, h1s, act, dgu, wdt, wnat, acc_gu, acc_d, own_send, own_recv, send, recv, out_sem,
):
    i = pl.program_id(0)
    x, c, y, z = place()
    me, far = 2 * x + c, 2 * (1 - x) + c
    to_core, to_x, to_y = device(x, 1 - c, y, z), device(1 - x, c, y, z), device(x, c, 1 - y, z)

    def lanes(s):
        return pl.ds(pl.multiple_of(128 * s, 128), 128)

    def piece(l, p, s, half):
        if isinstance(p, int) and p == 4:
            return wd.at[l, :, s, pl.ds(pl.multiple_of(16 * half, 16), 16), :]
        return wgu.at[l, pl.ds(pl.multiple_of(1408 * half + 352 * p, 32), 352), lanes(s)]

    def copy(l, p, stage):
        half = 1 - y if stage == 3 else y
        ref = piece(l, p, me if stage == 0 else far, half)
        return remote(ref, ref, send.at[l, p, stage], recv.at[l, p, stage], (to_x, to_y, to_core, to_core)[stage])

    def own(l, k):
        ref = wd.at[l, :, me] if k else wgu.at[l, :, lanes(me)]
        return remote(ref, ref, own_send.at[l, k], own_recv.at[l, k], to_core)

    def out_copies():
        return (
            pltpu.make_async_copy(wgu.at[0], wgu_out, out_sem.at[0]),
            pltpu.make_async_copy(wd.at[0], wd_out, out_sem.at[1]),
        )

    def from_x(l, p):
        copy(l, p, 0).wait_recv()
        copy(l, p, 1).start()
        copy(l, p, 2).start()

    def from_y(l, p):
        copy(l, p, 1).wait_recv()
        copy(l, p, 3).start()

    def arrived(l):
        for k in range(2):
            own(l, k).wait_recv()
        for p in range(5):
            for stage in (2, 3):
                copy(l, p, stage).wait_recv()

    def place_own(l):
        for g, ref in enumerate((gate_ref, up_ref)):
            turned = ref[l].T
            for n in range(UNITS):
                for s in range(4):
                    wgu[l, 256 * n + 128 * g + SEG * s : 256 * n + 128 * g + SEG * s + SEG, lanes(me)] = turned[
                        352 * s + SEG * n : 352 * s + SEG * n + SEG, :
                    ]
        wd[l, :, me] = down_ref[l].reshape(UNITS, SEG, D)

    @pl.when(i == 0)
    def _():
        greeted = greet((to_core, to_x, to_y))
        place_own(0)
        greeted()
        for l in range(2):
            if l:
                place_own(1)
            for k in range(2):
                own(l, k).start()
            for p in range(5):
                copy(l, p, 0).start()
        for p in range(5):
            from_x(0, p)
            if p:
                from_y(0, p - 1)
        from_y(0, 4)
        acc_gu[...] = jnp.zeros_like(acc_gu)
        acc_d[...] = jnp.zeros_like(acc_d)
        arrived(0)
        wdt[...] = wd[0].reshape(FF, D).T
        for one in out_copies():
            one.start()

    @pl.when((i >= 1) & (i <= 4))
    def _():
        from_x(1, i - 1)

    @pl.when((i >= 2) & (i <= 5))
    def _():
        from_y(1, i - 2)

    @pl.when(i == 5)
    def _():
        from_x(1, 4)

    @pl.when(i == 6)
    def _():
        from_y(1, 4)

    @pl.when(i == 8)
    def _():
        arrived(1)
        wnat[...] = wgu[1].T

    @pl.when(i < 8)
    def _():
        x = x_ref[...]
        wide = x.astype(F32)
        a = (wide * lax.rsqrt(jnp.mean(wide * wide, -1, keepdims=True) + 1e-6)).astype(BF)
        for n in range(UNITS):
            gu = nt(wgu[0, 256 * n : 256 * n + 256, :], a)
            act[128 * n : 128 * n + 128, :] = (gu[:128] * sigmoid(gu[:128]) * gu[128:]).astype(BF)
        h1s[i] = (x.T.astype(F32) + nn(wdt[...], act[...]).astype(BF).astype(F32)).astype(BF)

    @pl.when(i >= 8)
    def _():
        wide = h1s[i - 8].astype(F32)
        scale = lax.rsqrt(jnp.mean(wide * wide, 0, keepdims=True) + 1e-6)
        a = (wide * scale).astype(BF)
        dy = dy_ref[...]
        for n in range(UNITS):
            gu = nn(wgu[1, 256 * n : 256 * n + 256, :], a)
            d = nt(wd[1, n].reshape(128, D), dy).astype(BF).astype(F32)
            one, dg, du = backward_unit(gu[:128], gu[128:], d)
            act[128 * n : 128 * n + 128, :] = one
            dgu[256 * n : 256 * n + 128, :] = dg
            dgu[256 * n + 128 : 256 * n + 256, :] = du
        acc_d[...] += nn(act[...], dy)
        acc_gu[...] += nt(dgu[...], a)
        da = nn(wnat[...], dgu[...]).astype(BF).astype(F32)
        back = scale * da - wide * (scale * scale * scale * jnp.mean(wide * da, 0, keepdims=True))
        dh_ref[0] = (dy.T.astype(F32) + back.astype(BF).astype(F32)).astype(BF)

    @pl.when(i == 15)
    def _():
        @pl.loop(0, UNITS)
        def _(n):
            pack(n, acc_gu, acc_d, n, u_ref)

        for one in out_copies():
            one.wait()
        for l in range(2):
            for k in range(2):
                own(l, k).wait_send()
            for p in range(5):
                for stage in range(4):
                    copy(l, p, stage).wait_send()


def second_kernel(
    x_any, dh_any, wgu_any, wd_any, u_any, g_out, total_out,
    xs, a0, dh, wgu, wd, u, gu_s, d_s, act, dgu, acc_gu, acc_d,
    rc, sx, rx, sy, ry, sz, rz, g, sums, squares,
    s1, r1, s3, r3, norm_send, norm_recv, in_sem, tile_sem, out_sem,
):
    x, c, y, z = place()
    to_core, to_x, to_y = device(x, 1 - c, y, z), device(1 - x, c, y, z), device(x, c, 1 - y, z)
    to_z = [device(x, c, y, (z + k) % 4) for k in (1, 2, 3)]
    group = [to_core, to_x, device(1 - x, 1 - c, y, z)]
    greeted = greet([to_core, to_x, to_y, *to_z, group[2]])

    loads = [
        pltpu.make_async_copy(wgu_any, wgu, in_sem.at[0]),
        pltpu.make_async_copy(wd_any, wd, in_sem.at[1]),
        pltpu.make_async_copy(u_any, u.at[pl.ds(0, UNITS)], in_sem.at[2]),
    ]

    def tile_loads(t):
        rows = pl.ds(pl.multiple_of(TT * t, TT), TT)
        return pltpu.make_async_copy(x_any.at[rows], xs.at[t], tile_sem.at[t, 0]), pltpu.make_async_copy(dh_any.at[t], dh.at[t], tile_sem.at[t, 1])

    loads[0].start()
    for t in range(8):
        for one in tile_loads(t):
            one.start()
        if t == 0:
            loads[1].start()
            loads[2].start()
    squares[...] = jnp.zeros_like(squares)

    def c_copy(q):
        return remote(u.at[q, 1 - c], rc.at[q], s1.at[q, 0], r1.at[q, 0], to_core)

    def x_copy(q):
        return remote(sx.at[q], rx.at[q], s1.at[q, 1], r1.at[q, 1], to_x)

    def y_copy(q):
        return remote(sy.at[q], ry.at[q], s1.at[q, 2], r1.at[q, 2], to_y)

    def z_copy(q, k):
        return remote(sz.at[q, k], rz.at[q, k], s3.at[q, 0, k], r3.at[q, 0, k], to_z[k])

    def back_z_copy(q, k):
        return remote(g.at[q, 4 * y + z], g.at[q, 4 * y + z], s3.at[q, 1, k], r3.at[q, 1, k], to_z[k])

    def back_y_copy(q):
        half = g.at[q, pl.ds(4 * y, 4)]
        return remote(half, half, s1.at[q, 3], r1.at[q, 3], to_y)

    def upto_x(q, p):
        return u[q, c, x, p].astype(F32) + rc[q, x, p].astype(F32) + rx[q, p].astype(F32)

    def upto_y(q, k):
        return upto_x(q, 4 * y + k) + ry[q, k].astype(F32)

    def stage0(q):
        c_copy(q).start()

    def stage1(q):
        c_copy(q).wait_recv()
        sx[q] = (u[q, c, 1 - x].astype(F32) + rc[q, 1 - x].astype(F32)).astype(BF)
        x_copy(q).start()

    def stage2(q):
        x_copy(q).wait_recv()
        for k in range(4):
            sy[q, k] = upto_x(q, 4 * (1 - y) + k).astype(BF)
        y_copy(q).start()

    def stage3(q):
        y_copy(q).wait_recv()
        for k in range(3):
            sz[q, k] = upto_y(q, (z + k + 1) % 4).astype(BF)
        for k in range(3):
            z_copy(q, k).start()

    def stage4(q):
        for k in range(3):
            z_copy(q, k).wait_recv()
        total = upto_y(q, z)
        for k in range(3):
            total += rz[q, k].astype(F32)
        g[q, 4 * y + z] = total.astype(BF)
        for k in range(3):
            back_z_copy(q, k).start()

    def stage5(q):
        for k in range(3):
            back_z_copy(q, k).wait_recv()
        back_y_copy(q).start()

    def stage6(q):
        back_y_copy(q).wait_recv()
        wide = g[q].astype(F32).reshape(48, 8, 128)
        squares[...] += jnp.sum(wide * wide, 0)

    stages = (stage0, stage1, stage2, stage3, stage4, stage5, stage6)

    def tick(m):
        for j in reversed(range(7)):
            q = m - 2 * j

            @pl.when((q >= 0) & (q < ALL))
            def _():
                stages[j](q)

    for number, (first, units) in enumerate(CHUNKS):
        if number == 0:
            loads[0].wait()
            loads[1].wait()

        @pl.loop(0, 8)
        def _(t):
            if number == 0:
                for one in tile_loads(t):
                    one.wait()
                wide = xs[t].astype(F32)
                a0[t] = (wide * lax.rsqrt(jnp.mean(wide * wide, -1, keepdims=True) + 1e-6)).astype(BF)
            gu_s[: 256 * units, :] = nt(wgu[256 * first : 256 * (first + units), :], a0[t])
            d_s[: 128 * units, :] = nn(wd[first : first + units].reshape(128 * units, D), dh[t])
            for n in range(units):
                low = 256 * n
                one, dg, du = backward_unit(
                    gu_s[low : low + 128, :], gu_s[low + 128 : low + 256, :], d_s[128 * n : 128 * n + 128, :].astype(BF).astype(F32)
                )
                act[128 * n : 128 * n + 128, :] = one
                dgu[low : low + 128, :] = dg
                dgu[low + 128 : low + 256, :] = du
            new_d = nt(act[: 128 * units, :], dh[t])
            new_gu = nn(dgu[: 256 * units, :], a0[t])

            @pl.when(t == 0)
            def _():
                acc_d[: 128 * units, :] = new_d
                acc_gu[: 256 * units, :] = new_gu

            @pl.when(t > 0)
            def _():
                acc_d[: 128 * units, :] += new_d
                acc_gu[: 256 * units, :] += new_gu

            if number == 0:

                @pl.when(t == 1)
                def _():
                    greeted()
                    loads[2].wait()

            @pl.when(t % 2 == 1)
            def _():
                tick(4 * number + t // 2)

        @pl.loop(0, units)
        def _(n):
            pack(UNITS + first + n, acc_gu, acc_d, n, u)

    @pl.loop(16, ALL + 12)
    def _(m):
        tick(m)

    mine = sums.at[2 * x + c]
    norm = [remote(mine, mine, norm_send.at[k], norm_recv.at[k], group[k]) for k in range(3)]
    sums[2 * x + c] = squares[...]
    for one in norm:
        one.start()
    out = pltpu.make_async_copy(g, g_out, out_sem.at[0])
    out.start()

    @pl.loop(0, ALL)
    def _(q):
        for one in (c_copy(q), x_copy(q), y_copy(q), back_y_copy(q)):
            one.wait_send()
        for k in range(3):
            z_copy(q, k).wait_send()
            back_z_copy(q, k).wait_send()

    for one in norm:
        one.wait()
    total_out[...] = sums[0] + sums[1] + sums[2] + sums[3]
    out.wait()


def third_kernel(g_ref, total_ref, *refs):
    weights, ms, vs = refs[0:3], refs[3:6], refs[6:9]
    new_w, new_m, new_v = refs[9:12], refs[12:15], refs[15:18]
    turned, plain = refs[18:20]
    factor = jnp.minimum(1.0, 0.5 * lax.rsqrt(jnp.sum(total_ref[...]) / COUNT + 1e-30))

    def take(i, g):
        g = g * factor
        m = 0.9 * ms[i][0] + 0.1 * g
        v = 0.95 * vs[i][0] + 0.05 * g * g
        w = weights[i][0].astype(F32)
        new_m[i][0] = m
        new_v[i][0] = v
        new_w[i][0] = (w - 0.02 * (m * lax.rsqrt(v + 1e-8) + 0.1 * w)).astype(BF)

    for i in range(2):
        for n in range(UNITS):
            for s in range(4):
                turned[352 * s + SEG * n : 352 * s + SEG * n + SEG, :] = g_ref[0, n, 4 * i + s, 0:32, :].astype(F32)
        take(i, turned[...].T)
    for n in range(UNITS):
        for p in range(8):
            row = SEG * n + 16 * (p // 4)
            plain[row : row + 16, 128 * (p % 4) : 128 * (p % 4) + 128] = g_ref[0, n, p, 32:48, :].astype(F32)
    take(2, plain[...])


def step(x, dy, w_gate, w_up, w_down, *moments):
    tokens = x.shape[1]
    tiles = tokens // TT
    any_ = pl.BlockSpec(memory_space=pl.ANY)

    def once(shape):
        return pl.BlockSpec(shape, lambda i: (0,) * len(shape), pipeline_mode=pl.Buffered(1))

    unit = (UNITS, 2, 2, 8, 48, 128)
    dma = pltpu.SemaphoreType.DMA
    u1, dh, wgu0, wd0 = pl.pallas_call(
        first_kernel,
        grid=(2 * tiles,),
        in_specs=[
            pl.BlockSpec((TT, D), lambda i: (jnp.minimum(i, tiles - 1), 0)),
            pl.BlockSpec((TT, D), lambda i: (jnp.maximum(i - tiles, 0), 0)),
            once(w_gate.shape), once(w_up.shape), once(w_down.shape),
        ],
        out_specs=[once(unit), pl.BlockSpec((1, D, TT), lambda i: (jnp.maximum(i - tiles, 0), 0, 0)), any_, any_],
        out_shape=[
            jax.ShapeDtypeStruct(unit, BF),
            jax.ShapeDtypeStruct((tiles, D, TT), BF),
            jax.ShapeDtypeStruct((2 * FF, D), BF),
            jax.ShapeDtypeStruct((UNITS, 4, SEG, D), BF),
        ],
        scratch_shapes=[
            pltpu.VMEM((2, 2 * FF, D), BF),
            pltpu.VMEM((2, UNITS, 4, SEG, D), BF),
            pltpu.VMEM((tiles, D, TT), BF),
            pltpu.VMEM((FF, TT), BF),
            pltpu.VMEM((2 * FF, TT), BF),
            pltpu.VMEM((D, FF), BF),
            pltpu.VMEM((D, 2 * FF), BF),
            pltpu.VMEM((2 * FF, D), F32),
            pltpu.VMEM((FF, D), F32),
            dma((2, 2)), dma((2, 2)), dma((2, 5, 4)), dma((2, 5, 4)), dma((2,)),
        ],
        compiler_params=pltpu.CompilerParams(vmem_limit_bytes=VMEM_LIMIT, collective_id=0, has_side_effects=True),
        name="gather_forward_and_last_layer",
    )(x[0], dy[0], w_gate, w_up, w_down)

    most = max(units for _, units in CHUNKS)
    g, total = pl.pallas_call(
        second_kernel,
        in_specs=[any_] * 5,
        out_specs=[any_, pl.BlockSpec(memory_space=pltpu.VMEM)],
        out_shape=[jax.ShapeDtypeStruct((ALL, 8, 48, 128), BF), jax.ShapeDtypeStruct((8, 128), F32)],
        scratch_shapes=[
            pltpu.VMEM((tiles, TT, D), BF),
            pltpu.VMEM((tiles, TT, D), BF),
            pltpu.VMEM((tiles, D, TT), BF),
            pltpu.VMEM((2 * FF, D), BF),
            pltpu.VMEM((UNITS, 4, SEG, D), BF),
            pltpu.VMEM((ALL, 2, 2, 8, 48, 128), BF),
            pltpu.VMEM((256 * most, TT), F32),
            pltpu.VMEM((128 * most, TT), F32),
            pltpu.VMEM((128 * most, TT), BF),
            pltpu.VMEM((256 * most, TT), BF),
            pltpu.VMEM((256 * most, D), F32),
            pltpu.VMEM((128 * most, D), F32),
            pltpu.VMEM((ALL, 2, 8, 48, 128), BF),
            pltpu.VMEM((ALL, 8, 48, 128), BF),
            pltpu.VMEM((ALL, 8, 48, 128), BF),
            pltpu.VMEM((ALL, 4, 48, 128), BF),
            pltpu.VMEM((ALL, 4, 48, 128), BF),
            pltpu.VMEM((ALL, 3, 48, 128), BF),
            pltpu.VMEM((ALL, 3, 48, 128), BF),
            pltpu.VMEM((ALL, 8, 48, 128), BF),
            pltpu.VMEM((4, 8, 128), F32),
            pltpu.VMEM((8, 128), F32),
            dma((ALL, 4)), dma((ALL, 4)), dma((ALL, 2, 3)), dma((ALL, 2, 3)),
            dma((3,)), dma((3,)), dma((3,)), dma((tiles, 2)), dma((1,)),
        ],
        compiler_params=pltpu.CompilerParams(vmem_limit_bytes=VMEM_LIMIT, collective_id=1, has_side_effects=True),
        name="first_layer_and_sums",
    )(x[0], dh, wgu0, wd0, u1)

    arrays = (w_gate, w_up, w_down, *moments)

    def by_layer(a):
        return pl.BlockSpec((1,) + a.shape[1:], lambda l: (l, 0, 0))

    return pl.pallas_call(
        third_kernel,
        grid=(2,),
        in_specs=[pl.BlockSpec((1, UNITS, 8, 48, 128), lambda l: (1 - l, 0, 0, 0, 0)), pl.BlockSpec((8, 128), lambda l: (0, 0))]
        + [by_layer(a) for a in arrays],
        out_specs=[by_layer(a) for a in arrays],
        out_shape=[jax.ShapeDtypeStruct(a.shape, a.dtype) for a in arrays],
        scratch_shapes=[pltpu.VMEM((FF, 128), F32), pltpu.VMEM((FF // 4, D), F32)],
        compiler_params=pltpu.CompilerParams(vmem_limit_bytes=VMEM_LIMIT),
        name="clip_and_adamw",
    )(g.reshape(2, UNITS, 8, 48, 128), total, *arrays)


def solution(mesh):
    states, cut = P(("rep", "r", "s"), None, None), P(None, "s", None)
    return jax.shard_map(
        lambda *arrays: tuple(step(*arrays)),
        mesh=mesh,
        in_specs=(states, states) + (cut,) * 9,
        out_specs=(P("rep", "s", None),) * 9,
        check_vma=False,
    )
```

time: 542 us -> 238 us (0.44); the launches traced: 533 us -> 238 us
  matrix products: 249 us -> 0 us
  Pallas kernels: 0 us -> 237 us
  waiting for transfers between devices: 219 us -> 0 us
  other arithmetic: 20.6 us -> 0 us
  local copies, waits for them, and re-layouts: 18.8 us -> 0 us
  between operations: 17 us -> 0.82 us
  blocking collectives: 6.83 us -> 0 us
    dot_general x15 -> x0, matrix products: 249 us -> none  [the longest x5 93.4 us: layer(): gate = jnp.dot(a, w['w_gate'], preferred_element_type=jnp.float32)]
    pallas_call x0 -> x3, Pallas kernels: none -> 237 us  [the longest x1 118 us: step(): pl.pallas_call(first_kernel, grid=(2 * tiles,), in_specs=[pl.BlockSpec((T...]
    psum x1 -> x0, waiting for transfers between devices: 108 us -> none  [summed(): lax.psum(lax.psum_scatter(term, 's', scatter_dimension=0, tiled=True), 'r')]
    reduce_scatter x6 -> x0, waiting for transfers between devices: 80 us -> none  [summed(): lax.psum_scatter(term, 's', scatter_dimension=0, tiled=True)]
    all_gather x6 -> x0, waiting for transfers between devices: 29.4 us -> none  [fetched(): lax.all_gather(w[number], 's', axis=0, tiled=True)]
    unnamed x40 -> x0, local copies, waits for them, and re-layouts: 12.8 us -> none
    reduce_sum x4 -> x0, other arithmetic: 9.42 us -> none  [the longest x3 6.36 us: step(): squares = lax.psum(sum((jnp.sum(g * g) for g in gradients)), 's')]
    convert_element_type x2 -> x0, other arithmetic: 8.25 us -> none  [adamw(): return ((w - 0.02 * step).astype(jnp.bfloat16), m, v)]
  transfers between devices with their start and end apart: 13 -> 0, of which waited for: 9 -> 0; matrix products, arithmetic and copies ran while one was open for 43% -> 0% of each run, Pallas kernels for 0% -> 0%
where the time goes in v1:
time: 238 us
  Pallas kernels  237 us (100%)
    pallas_call x1, Pallas kernels, step(): pl.pallas_call(first_kernel, grid=(2 * tiles,), in_specs=[pl.BlockSpec((T...  118 us
    pallas_call x1, Pallas kernels, step(): pl.pallas_call(second_kernel, in_specs=[any_] * 5, out_specs=[any_, pl.Bl...  111 us
    pallas_call x1, Pallas kernels, step(): pl.pallas_call(third_kernel, grid=(2,), in_specs=[pl.BlockSpec((1, UNITS,...  8.45 us

profile of v1, /device:TPU:0, one launch (start us, length us, event | category | flops | bytes accessed | tf_op | source)
XLA Modules:
  0.0 238.0 jit_solution(13089827488668782814)
XLA Ops:
  0.6 117.8 %gather_forward_and_last_layer.1 = (bf16[11,2,2,8,48,128]{5,4,3,2,1,0:T(8,128)(2,1)}, bf16[8,512,512]{2,1,0:T(8,128)(2,1)}, bf16[2816,512]{1,0:T(8,128)(2,1)}, bf16[11,4,32,512]{3,2,1,0:T(8,128)(2,1)}) custom-call(bf16[4096,512]{1,0:T(8,128)(2,1)} %bitcast.3, bf16[4096,512]{1,0:T(8,128)(2,1)} %bitcast.5, bf16[2,128,1408]{2,1,0:T(8,128)(2,1)} %refs_0_.1, ...), custom_call_target="tpu_custom_call" | custom-call | tf_op jit(solution)/shard_map/gather_forward_and_last_layer/pallas_call | solution.py:439
  118.4 111.0 %first_layer_and_sums.1 = (bf16[22,8,48,128]{3,2,1,0:T(8,128)(2,1)}, f32[8,128]{1,0:T(8,128)}) custom-call(bf16[4096,512]{1,0:T(8,128)(2,1)} %bitcast.4, bf16[8,512,512]{2,1,0:T(8,128)(2,1)} %get-tuple-element.15.dh_any, bf16[2816,512]{1,0:T(8,128)(2,1)} %get-tuple-element.16.wgu_any, bf16[11,4,32,512]{3,2,1,0:T(8,128)(2,1)} %get-tuple-element.17.wd_any, ...), custom_call_target="tpu_custom_call" | custom-call | tf_op jit(solution)/shard_map/first_layer_and_sums/pallas_call | solution.py:471
  229.4 8.4 %clip_and_adamw.1 = (bf16[2,128,1408]{2,1,0:T(8,128)(2,1)}, bf16[2,128,1408]{2,1,0:T(8,128)(2,1)}, bf16[2,352,512]{2,1,0:T(8,128)(2,1)}, f32[2,128,1408]{2,1,0:T...) custom-call(bf16[2,11,8,48,128]{4,3,2,1,0:T(8,128)(2,1)} %bitcast.6,, ...), custom_call_target="tpu_custom_call" | custom-call | tf_op jit(solution)/shard_map/clip_and_adamw/pallas_call | solution.py:511

commit v2 on v1

v2 whole, which is shorter than its diff:
```python
import functools

import jax
import jax.numpy as jnp
from jax import lax
from jax.experimental import pallas as pl
from jax.experimental.pallas import tpu as pltpu
from jax.sharding import PartitionSpec as P

F32, BF = jnp.float32, jnp.bfloat16
D, FF, TT, WIDE = 512, 1408, 512, 1024
UNITS, SEG = 11, 32
ALL = 2 * UNITS
CHUNKS = ((0, 3), (3, 3), (6, 3), (9, 2))
COUNT = 2 * 3 * D * FF
MIB = 2**20
VMEM_LIMIT = 62 * MIB
LANE, PAIR = 128, 256


def nn(a, b):
    return lax.dot_general(a, b, (((1,), (0,)), ((), ())), preferred_element_type=F32)


def nt(a, b):
    return lax.dot_general(a, b, (((1,), (1,)), ((), ())), preferred_element_type=F32)


def sigmoid(g):
    return 0.5 * jnp.tanh(0.5 * g) + 0.5


def backward_unit(g, u, d):
    s = sigmoid(g)
    silu = g * s
    return (silu * u).astype(BF), (d * u * (s + silu * (1.0 - s))).astype(BF), (d * silu).astype(BF)


def place():
    r, s = lax.axis_index("r"), lax.axis_index("s")
    return s // 2, s % 2, r // 4, r % 4


def device(x, core, y, z):
    return (0, y * 4 + z, x * 2 + core)


def remote(src, dst, send, recv, where):
    return pltpu.make_async_remote_copy(
        src_ref=src, dst_ref=dst, send_sem=send, recv_sem=recv, device_id=where, device_id_type=pl.DeviceIdType.MESH
    )


def greet(peers):
    barrier = pltpu.get_barrier_semaphore()
    for peer in peers:
        pl.semaphore_signal(barrier, inc=1, device_id=peer, device_id_type=pl.DeviceIdType.MESH)
    return lambda: pl.semaphore_wait(barrier, len(peers))


def pack(n, acc_gu, acc_d, row, out):
    for core in range(2):
        for x in range(2):
            s = 2 * x + core
            for p in range(8):
                y, z = p // 4, p % 4
                gu = pl.ds(pl.multiple_of(PAIR * row + 32 * p, 32), 32)
                d = pl.ds(pl.multiple_of(LANE * row + SEG * s + 16 * y, 16), 16)
                out[n, core, x, p, 0:32, :] = acc_gu[gu, LANE * s : LANE * s + LANE].astype(BF)
                out[n, core, x, p, 32:48, :] = acc_d[d, LANE * z : LANE * z + LANE].astype(BF)


def first_kernel(
    x_ref, dy_ref, gate_ref, up_ref, down_ref, u_ref, dh_ref, gu_out, wd_out,
    wgu, wd, h1s, acts, a_first, stage, dgu, wdt, acc_gu, acc_d, own_send, own_recv, send, recv, gu_sem, out_sem,
):
    i = pl.program_id(0)
    x, c, y, z = place()
    me, far = 2 * x + c, 2 * (1 - x) + c
    to_core, to_x, to_y = device(x, 1 - c, y, z), device(1 - x, c, y, z), device(x, c, 1 - y, z)

    def lanes(s):
        return pl.ds(pl.multiple_of(LANE * s, LANE), LANE)

    def piece(l, p, s, half):
        if p == 4:
            return wd.at[l, :, s, pl.ds(pl.multiple_of(16 * half, 16), 16), :]
        first, units = CHUNKS[p]
        return wgu.at[l, pl.ds(first, units), half, :, lanes(s)]

    def copy(l, p, stage):
        half = 1 - y if stage == 3 else y
        ref = piece(l, p, me if stage == 0 else far, half)
        return remote(ref, ref, send.at[l, p, stage], recv.at[l, p, stage], (to_x, to_y, to_core, to_core)[stage])

    def own(l, k):
        ref = wd.at[l, :, me] if k else wgu.at[l, :, :, :, lanes(me)]
        return remote(ref, ref, own_send.at[l, k], own_recv.at[l, k], to_core)

    wd_copy = pltpu.make_async_copy(wd, wd_out, out_sem.at[0])

    def gu_copy(p, t):
        first, units = CHUNKS[p]
        rows = pl.ds(first, units)
        there = gu_out.at[rows, t // 2, :, pl.ds(pl.multiple_of(TT * (t % 2), TT), TT)]
        return pltpu.make_async_copy(stage.at[t % 2, rows], there, gu_sem.at[p, t % 2])

    def from_x(l, p):
        copy(l, p, 0).wait_recv()
        copy(l, p, 1).start()
        copy(l, p, 2).start()

    def from_y(l, p):
        copy(l, p, 1).wait_recv()
        copy(l, p, 3).start()

    def arrived(l, p):
        for stage in (2, 3):
            copy(l, p, stage).wait_recv()

    def place_own(l):
        for g, ref in enumerate((gate_ref, up_ref)):
            turned = ref[l].T
            for n in range(UNITS):
                for s in range(4):
                    wgu[l, n, g, SEG * s : SEG * s + SEG, lanes(me)] = turned[
                        352 * s + SEG * n : 352 * s + SEG * n + SEG, :
                    ]
        wd[l, :, me] = down_ref[l].reshape(UNITS, SEG, D)

    def up_and_gate(first, units, a, out, slot):
        for n in range(first, first + units):
            gu = nt(wgu[0, n].reshape(PAIR, D), a)
            stage[slot, n] = gu
            out[LANE * n : LANE * n + LANE, :] = (gu[:LANE] * sigmoid(gu[:LANE]) * gu[LANE:]).astype(BF)

    def down(x, act, t):
        h1s[t] = (x.T.astype(F32) + nn(wdt[...], act[...]).astype(BF).astype(F32)).astype(BF)

    @pl.when(i == 0)
    def _():
        greeted = greet((to_core, to_x, to_y))
        place_own(0)
        greeted()
        for l in range(2):
            if l:
                place_own(1)
            for k in range(2):
                own(l, k).start()
            for p in range(5):
                copy(l, p, 0).start()
        acc_gu[...] = jnp.zeros_like(acc_gu)
        acc_d[...] = jnp.zeros_like(acc_d)
        own(0, 0).wait_recv()
        from_x(0, 0)
        for p in range(4):
            from_x(0, p + 1)
            from_y(0, p)
            arrived(0, p)
            first, units = CHUNKS[p]

            @pl.loop(0, 4)
            def _(t):
                if p == 0:
                    wide = x_ref[t].astype(F32)
                    a_first[t] = (wide * lax.rsqrt(jnp.mean(wide * wide, -1, keepdims=True) + 1e-6)).astype(BF)

                @pl.when(t >= 2)
                def _():
                    gu_copy(p, t - 2).wait()

                up_and_gate(first, units, a_first[t], acts.at[t], t % 2)
                gu_copy(p, t).start()

        from_y(0, 4)
        own(0, 1).wait_recv()
        arrived(0, 4)
        wdt[...] = wd[0].reshape(FF, D).T

        @pl.loop(0, 4)
        def _(t):
            for p in range(4):

                @pl.when(t == p)
                def _():
                    from_x(1, p)

            down(x_ref[t], acts.at[t], t)

    @pl.when(i == 1)
    def _():
        @pl.loop(0, 4)
        def _(t):
            @pl.when(t == 0)
            def _():
                from_y(1, 0)
                from_y(1, 1)

            @pl.when(t == 1)
            def _():
                from_x(1, 4)
                from_y(1, 2)

            @pl.when(t == 2)
            def _():
                from_y(1, 3)

            @pl.when(t == 3)
            def _():
                from_y(1, 4)

            x = x_ref[t]
            wide = x.astype(F32)
            a = (wide * lax.rsqrt(jnp.mean(wide * wide, -1, keepdims=True) + 1e-6)).astype(BF)
            for p in range(4):
                gu_copy(p, t + 2).wait()
            up_and_gate(0, UNITS, a, acts.at[0], t % 2)
            for p in range(4):
                gu_copy(p, t + 4).start()
            down(x, acts.at[0], 4 + t)

        for k in range(2):
            own(1, k).wait_recv()
        for p in range(5):
            arrived(1, p)
        wd_copy.start()

    @pl.when(i >= 2)
    def _():
        act = acts.at[0]
        wide = h1s[i - 2].astype(F32)
        scale = lax.rsqrt(jnp.mean(wide * wide, 0, keepdims=True) + 1e-6)
        a = (wide * scale).astype(BF)
        dy = dy_ref[...]
        dyt = dy.T
        for n in range(UNITS):
            gu = nn(wgu[1, n].reshape(PAIR, D), a)
            d = nn(wd[1, n].reshape(LANE, D), dyt).astype(BF).astype(F32)
            one, dg, du = backward_unit(gu[:LANE], gu[LANE:], d)
            act[LANE * n : LANE * n + LANE, :] = one
            dgu[PAIR * n : PAIR * n + LANE, :] = dg
            dgu[PAIR * n + LANE : PAIR * n + PAIR, :] = du
        acc_d[...] += nn(act[...], dy)
        acc_gu[...] += nt(dgu[...], a)
        da = lax.dot_general(wgu[1].reshape(2 * FF, D), dgu[...], (((0,), (0,)), ((), ())), preferred_element_type=F32).astype(BF).astype(F32)
        back = scale * da - wide * (scale * scale * scale * jnp.mean(wide * da, 0, keepdims=True))
        dh_ref[0] = (dyt.astype(F32) + back.astype(BF).astype(F32)).astype(BF)

    @pl.when(i == 9)
    def _():
        @pl.loop(0, UNITS)
        def _(n):
            pack(n, acc_gu, acc_d, n, u_ref)

        wd_copy.wait()
        for p in range(4):
            for t in (6, 7):
                gu_copy(p, t).wait()
        for l in range(2):
            for k in range(2):
                own(l, k).wait_send()
            for p in range(5):
                for stage in range(4):
                    copy(l, p, stage).wait_send()


def second_kernel(
    x_any, dh_any, gu_any, wd_any, u_any, g_out, total_out,
    a0, dh, gu, wd, u, act, dgu, acc_gu, acc_d,
    rc, sx, rx, sy, ry, sz, rz, g, sums, squares,
    s1, r1, s3, r3, norm_send, norm_recv, in_sem, tile_sem,
):
    x, c, y, z = place()
    to_core, to_x, to_y = device(x, 1 - c, y, z), device(1 - x, c, y, z), device(x, c, 1 - y, z)
    to_z = [device(x, c, y, (z + k) % 4) for k in (1, 2, 3)]
    group = [to_core, to_x, device(1 - x, 1 - c, y, z)]
    greeted = greet([to_core, to_x, to_y, *to_z, group[2]])

    wd_load = pltpu.make_async_copy(wd_any.at[0], wd, in_sem.at[2])

    def own_load(k):
        units = pl.ds(k, 1) if k == 0 else pl.ds(1, UNITS - 1)
        return pltpu.make_async_copy(u_any.at[units], u.at[units], in_sem.at[3 + k])

    def gu_load(k, t):
        first, units = CHUNKS[k]
        return pltpu.make_async_copy(gu_any.at[pl.ds(first, units), t], gu.at[t % 2, pl.ds(0, units)], in_sem.at[t % 2])

    def tile_loads(t):
        rows = pl.ds(WIDE * t, WIDE)
        return pltpu.make_async_copy(x_any.at[rows], a0.at[t], tile_sem.at[t, 0]), pltpu.make_async_copy(dh_any.at[t], dh.at[t], tile_sem.at[t, 1])

    for one in (own_load(0), own_load(1), wd_load, gu_load(0, 0), *tile_loads(0)):
        one.start()
    for t in range(1, 4):
        for one in tile_loads(t):
            one.start()
    squares[...] = jnp.zeros_like(squares)

    def c_copy(q):
        return remote(u.at[q, 1 - c], rc.at[q], s1.at[q, 0], r1.at[q, 0], to_core)

    def x_copy(q):
        return remote(sx.at[q], rx.at[q], s1.at[q, 1], r1.at[q, 1], to_x)

    def y_copy(q):
        return remote(sy.at[q], ry.at[q], s1.at[q, 2], r1.at[q, 2], to_y)

    def z_copy(q, k):
        return remote(sz.at[q, k], rz.at[q, k], s3.at[q, 0, k], r3.at[q, 0, k], to_z[k])

    def back_z_copy(q, k):
        return remote(g.at[q, 4 * y + z], g.at[q, 4 * y + z], s3.at[q, 1, k], r3.at[q, 1, k], to_z[k])

    def back_y_copy(q):
        half = g.at[q, pl.ds(4 * y, 4)]
        return remote(half, half, s1.at[q, 3], r1.at[q, 3], to_y)

    def upto_x(q, p):
        return u[q, c, x, p].astype(F32) + rc[q, x, p].astype(F32) + rx[q, p].astype(F32)

    def upto_y(q, k):
        return upto_x(q, 4 * y + k) + ry[q, k].astype(F32)

    def stage0(q):
        c_copy(q).start()

    def stage1(q):
        c_copy(q).wait_recv()
        sx[q] = (u[q, c, 1 - x].astype(F32) + rc[q, 1 - x].astype(F32)).astype(BF)
        x_copy(q).start()

    def stage2(q):
        x_copy(q).wait_recv()
        for k in range(4):
            sy[q, k] = upto_x(q, 4 * (1 - y) + k).astype(BF)
        y_copy(q).start()

    def stage3(q):
        y_copy(q).wait_recv()
        for k in range(3):
            sz[q, k] = upto_y(q, (z + k + 1) % 4).astype(BF)
        for k in range(3):
            z_copy(q, k).start()

    def stage4(q):
        for k in range(3):
            z_copy(q, k).wait_recv()
        total = upto_y(q, z)
        for k in range(3):
            total += rz[q, k].astype(F32)
        g[q, 4 * y + z] = total.astype(BF)
        for k in range(3):
            back_z_copy(q, k).start()

    def stage5(q):
        for k in range(3):
            back_z_copy(q, k).wait_recv()
        back_y_copy(q).start()

    def stage6(q):
        back_y_copy(q).wait_recv()
        wide = g[q].astype(F32).reshape(48, 8, LANE)
        squares[...] += jnp.sum(wide * wide, 0)

    stages = (stage0, stage1, stage2, stage3, stage4, stage5, stage6)

    def tick(m):
        for j in reversed(range(7)):
            q = m - max(2 * j - 1, 0)

            @pl.when((q >= 0) & (q < ALL))
            def _():
                stages[j](q)

    own_load(0).wait()
    greeted()
    tick(0)
    own_load(1).wait()
    wd_load.wait()
    for number, (first, units) in enumerate(CHUNKS):
        acc_d[...] = jnp.zeros_like(acc_d)
        acc_gu[...] = jnp.zeros_like(acc_gu)

        @pl.loop(0, 4)
        def _(t):
            @pl.when(t < 3)
            def _():
                gu_load(number, t + 1).start()

            if number < 3:

                @pl.when(t == 3)
                def _():
                    gu_load(number + 1, 0).start()

            gu_load(number, t).wait()
            if number == 0:
                for one in tile_loads(t):
                    one.wait()
                wide = a0[t].astype(F32)
                a0[t] = (wide * lax.rsqrt(jnp.mean(wide * wide, -1, keepdims=True) + 1e-6)).astype(BF)
            a, h = a0[t], dh[t]
            for n in range(units):
                d = nn(wd[first + n].reshape(LANE, D), h).astype(BF).astype(F32)
                one, dg, du = backward_unit(gu[t % 2, n, :LANE, :], gu[t % 2, n, LANE:, :], d)
                act[LANE * n : LANE * n + LANE, :] = one
                dgu[PAIR * n : PAIR * n + LANE, :] = dg
                dgu[PAIR * n + LANE : PAIR * n + PAIR, :] = du
            acc_d[: LANE * units, :] += nt(act[: LANE * units, :], h)
            acc_gu[: PAIR * units, :] += nn(dgu[: PAIR * units, :], a)

            tick(5 * number + t + 1)

        @pl.loop(0, units)
        def _(n):
            pack(UNITS + first + n, acc_gu, acc_d, n, u)

        tick(5 * number + 5)

    @pl.loop(21, ALL + 11)
    def _(m):
        tick(m)

    mine = sums.at[2 * x + c]
    norm = [remote(mine, mine, norm_send.at[k], norm_recv.at[k], group[k]) for k in range(3)]
    sums[2 * x + c] = squares[...]
    for one in norm:
        one.start()
    g_out[...] = g[...]

    @pl.loop(0, ALL)
    def _(q):
        for one in (c_copy(q), x_copy(q), y_copy(q), back_y_copy(q)):
            one.wait_send()
        for k in range(3):
            z_copy(q, k).wait_send()
            back_z_copy(q, k).wait_send()

    for one in norm:
        one.wait()
    total_out[...] = sums[0] + sums[1] + sums[2] + sums[3]


def third_kernel(g_ref, total_ref, *refs):
    weights, ms, vs = refs[0:3], refs[3:6], refs[6:9]
    outs, buffers = refs[9:18], refs[18:27]
    turned, plain, sem = refs[27:30]
    factor = jnp.minimum(1.0, 0.5 * lax.rsqrt(jnp.sum(total_ref[...]) / COUNT + 1e-30))

    def copies(l, i):
        return [pltpu.make_async_copy(buffers[k].at[l], outs[k].at[l], sem.at[l, k]) for k in (i, 3 + i, 6 + i)]

    def take(l, i, g):
        g = g * factor
        m = 0.9 * ms[i][l] + 0.1 * g
        v = 0.95 * vs[i][l] + 0.05 * g * g
        w = weights[i][l].astype(F32)
        buffers[3 + i][l] = m
        buffers[6 + i][l] = v
        buffers[i][l] = (w - 0.02 * (m * lax.rsqrt(v + 1e-8) + 0.1 * w)).astype(BF)
        for one in copies(l, i):
            one.start()

    for l in range(2):
        for n in range(UNITS):
            for p in range(8):
                row = SEG * n + 16 * (p // 4)
                plain[row : row + 16, LANE * (p % 4) : LANE * (p % 4) + LANE] = g_ref[1 - l, n, p, 32:48, :].astype(F32)
        take(l, 2, plain[...])
        for i in range(2):
            for n in range(UNITS):
                for s in range(4):
                    turned[352 * s + SEG * n : 352 * s + SEG * n + SEG, :] = g_ref[1 - l, n, 4 * i + s, 0:32, :].astype(F32)
            take(l, i, turned[...].T)
    for l in range(2):
        for i in range(3):
            for one in copies(l, i):
                one.wait()


def step(x, dy, w_gate, w_up, w_down, *moments):
    tokens = x.shape[1]
    tiles = tokens // TT
    any_ = pl.BlockSpec(memory_space=pl.ANY)

    def once(shape):
        return pl.BlockSpec(shape, lambda i: (0,) * len(shape), pipeline_mode=pl.Buffered(1))

    unit = (UNITS, 2, 2, 8, 48, LANE)
    dma = pltpu.SemaphoreType.DMA
    u1, dh, gu0, wd0 = pl.pallas_call(
        first_kernel,
        grid=(2 + tiles,),
        in_specs=[
            pl.BlockSpec((tiles // 2, TT, D), lambda i: (jnp.minimum(i, 1), 0, 0)),
            pl.BlockSpec((TT, D), lambda i: (jnp.maximum(i - 2, 0), 0)),
            once(w_gate.shape), once(w_up.shape), once(w_down.shape),
        ],
        out_specs=[once(unit), pl.BlockSpec((1, D, TT), lambda i: (jnp.maximum(i - 2, 0) // 2, 0, jnp.maximum(i - 2, 0) % 2)), any_, any_],
        out_shape=[
            jax.ShapeDtypeStruct(unit, BF),
            jax.ShapeDtypeStruct((tiles // 2, D, WIDE), BF),
            jax.ShapeDtypeStruct((UNITS, tiles // 2, PAIR, WIDE), F32),
            jax.ShapeDtypeStruct((2, UNITS, 4, SEG, D), BF),
        ],
        scratch_shapes=[
            pltpu.VMEM((2, UNITS, 2, LANE, D), BF),
            pltpu.VMEM((2, UNITS, 4, SEG, D), BF),
            pltpu.VMEM((tiles, D, TT), BF),
            pltpu.VMEM((tiles // 2, FF, TT), BF),
            pltpu.VMEM((tiles // 2, TT, D), BF),
            pltpu.VMEM((2, UNITS, PAIR, TT), F32),
            pltpu.VMEM((2 * FF, TT), BF),
            pltpu.VMEM((D, FF), BF),
            pltpu.VMEM((2 * FF, D), F32),
            pltpu.VMEM((FF, D), F32),
            dma((2, 2)), dma((2, 2)), dma((2, 5, 4)), dma((2, 5, 4)), dma((4, 2)), dma((1,)),
        ],
        compiler_params=pltpu.CompilerParams(vmem_limit_bytes=VMEM_LIMIT, collective_id=0, has_side_effects=True),
        name="gather_forward_and_last_layer",
    )(x.reshape(tiles, TT, D), dy[0], w_gate, w_up, w_down)

    most = max(units for _, units in CHUNKS)
    g, total = pl.pallas_call(
        second_kernel,
        in_specs=[pl.BlockSpec(memory_space=pltpu.HBM)] * 5,
        out_specs=[pl.BlockSpec(memory_space=pltpu.VMEM)] * 2,
        out_shape=[jax.ShapeDtypeStruct((ALL, 8, 48, LANE), BF), jax.ShapeDtypeStruct((8, LANE), F32)],
        scratch_shapes=[
            pltpu.VMEM((tiles // 2, WIDE, D), BF),
            pltpu.VMEM((tiles // 2, D, WIDE), BF),
            pltpu.VMEM((2, most, PAIR, WIDE), F32),
            pltpu.VMEM((UNITS, 4, SEG, D), BF),
            pltpu.VMEM((ALL, 2, 2, 8, 48, LANE), BF),
            pltpu.VMEM((LANE * most, WIDE), BF),
            pltpu.VMEM((PAIR * most, WIDE), BF),
            pltpu.VMEM((PAIR * most, D), F32),
            pltpu.VMEM((LANE * most, D), F32),
            pltpu.VMEM((ALL, 2, 8, 48, LANE), BF),
            pltpu.VMEM((ALL, 8, 48, LANE), BF),
            pltpu.VMEM((ALL, 8, 48, LANE), BF),
            pltpu.VMEM((ALL, 4, 48, LANE), BF),
            pltpu.VMEM((ALL, 4, 48, LANE), BF),
            pltpu.VMEM((ALL, 3, 48, LANE), BF),
            pltpu.VMEM((ALL, 3, 48, LANE), BF),
            pltpu.VMEM((ALL, 8, 48, LANE), BF),
            pltpu.VMEM((4, 8, LANE), F32),
            pltpu.VMEM((8, LANE), F32),
            dma((ALL, 4)), dma((ALL, 4)), dma((ALL, 2, 3)), dma((ALL, 2, 3)),
            dma((3,)), dma((3,)), dma((5,)), dma((tiles, 2)),
        ],
        compiler_params=pltpu.CompilerParams(vmem_limit_bytes=50 * MIB, collective_id=1, has_side_effects=True),
        name="first_layer_and_sums",
    )(x[0], dh, gu0, wd0, u1)

    arrays = (w_gate, w_up, w_down, *moments)

    vmem = pl.BlockSpec(memory_space=pltpu.VMEM)
    return pl.pallas_call(
        third_kernel,
        in_specs=[vmem] * (2 + len(arrays)),
        out_specs=[any_] * len(arrays),
        out_shape=[jax.ShapeDtypeStruct(a.shape, a.dtype) for a in arrays],
        scratch_shapes=[pltpu.VMEM(a.shape, a.dtype) for a in arrays]
        + [pltpu.VMEM((FF, LANE), F32), pltpu.VMEM((FF // 4, D), F32), dma((2, 9))],
        compiler_params=pltpu.CompilerParams(vmem_limit_bytes=28 * MIB),
        name="clip_and_adamw",
    )(g.reshape(2, UNITS, 8, 48, LANE), total, *arrays)


def solution(mesh):
    states, cut = P(("rep", "r", "s"), None, None), P(None, "s", None)
    return jax.shard_map(
        lambda *arrays: tuple(step(*arrays)),
        mesh=mesh,
        in_specs=(states, states) + (cut,) * 9,
        out_specs=(P("rep", "s", None),) * 9,
        check_vma=False,
    )
```

time: 238 us -> 206 us (0.87)
  Pallas kernels: 237 us -> 205 us
    pallas_call x3, Pallas kernels: 237 us -> 205 us  [the longest x1 112 us: step(): pl.pallas_call(first_kernel, grid=(2 + tiles,), in_specs=[pl.BlockSpec((t...]
where the time goes in v2:
time: 206 us
  Pallas kernels  205 us (100%)
    pallas_call x1, Pallas kernels, step(): pl.pallas_call(first_kernel, grid=(2 + tiles,), in_specs=[pl.BlockSpec((t...  112 us
    pallas_call x1, Pallas kernels, step(): pl.pallas_call(second_kernel, in_specs=[pl.BlockSpec(memory_space=pltpu.H...  86.1 us
    pallas_call x1, Pallas kernels, step(): pl.pallas_call(third_kernel, in_specs=[vmem] * (2 + len(arrays)), out_spe...  6.23 us

profile of v2, /device:TPU:0, one launch (start us, length us, event | category | flops | bytes accessed | tf_op | source)
XLA Modules:
  0.0 205.6 jit_solution(2073958661837980696)
XLA Ops:
  0.6 112.3 %gather_forward_and_last_layer.1 = (bf16[11,2,2,8,48,128]{5,4,3,2,1,0:T(8,128)(2,1)}, bf16[4,512,1024]{2,1,0:T(8,128)(2,1)}, f32[11,4,256,1024]{3,2,1,0:T(8,128)}, bf16[2,11,4,32,512]{4,3,2,1,0:T(8,128)(2,1)}) custom-call(bf16[8,512,512]{2,1,0:T(8,128)(2,1)} %bitcast.5, bf16[4096,512]{1,0:T(8,128)(2,1)} %bitcast.7, bf16[2,128,1408]{2,1,0:T(8,128)(2,1)} %refs_0_.1, ...), custom_call_target="tpu_custom_call" | custom-call | tf_op jit(solution)/shard_map/gather_forward_and_last_layer/pallas_call | solution.py:492
  112.9 0.0 copy-start
  112.9 0.0 copy-start.1
  112.9 0.0 copy-start.2
  113.0 0.0 copy-start.3
  113.0 0.0 copy-start.4
  113.0 0.0 copy-start.5
  113.0 0.0 copy-start.6
  113.0 0.0 copy-start.7
  113.0 0.0 copy-start.8
  113.0 86.1 %first_layer_and_sums.1 = (bf16[22,8,48,128]{3,2,1,0:T(8,128)(2,1)S(1)}, f32[8,128]{1,0:T(8,128)S(1)}) custom-call(bf16[4096,512]{1,0:T(8,128)(2,1)} %bitcast.6, bf16[4,512,1024]{2,1,0:T(8,128)(2,1)} %get-tuple-element.15.dh_any, f32[11,4,256,1024]{3,2,1,0:T(8,128)} %get-tuple-element.16.gu_any, bf16[2,11,4,32,512]{4,3,2,1,0:T(8,128)(2,1)} %get-tuple-element.17.wd_any, ...), custom_call_target="tpu_custom_call" | custom-call | tf_op jit(solution)/shard_map/first_layer_and_sums/pallas_call | solution.py:525
  199.1 0.0 copy-done
  199.1 0.0 copy-done.1
  199.1 0.0 copy-done.2
  199.1 0.0 copy-done.3
  199.1 0.0 copy-done.4
  199.2 0.0 copy-done.5
  199.2 0.0 copy-done.6
  199.2 0.0 copy-done.7
  199.2 0.0 copy-done.8
  199.2 6.2 %clip_and_adamw.1 = (bf16[2,128,1408]{2,1,0:T(8,128)(2,1)}, bf16[2,128,1408]{2,1,0:T(8,128)(2,1)}, bf16[2,352,512]{2,1,0:T(8,128)(2,1)}, f32[2,128,1408]{2,1,0:T...) custom-call(bf16[2,11,8,48,128]{4,3,2,1,0:T(8,128)(2,1)S(1)} %bitcas, ...), custom_call_target="tpu_custom_call" | custom-call | tf_op jit(solution)/shard_map/clip_and_adamw/pallas_call | solution.py:560
Async XLA Ops:
  112.9 86.2 %copy-start = (bf16[2,128,1408]{2,1,0:T(8,128)(2,1)S(1)}, bf16[2,128,1408]{2,1,0:T(8,128)(2,1)}, u32[]{:S(2)}) copy-start(bf16[2,128,1408]{2,1,0:T(8,128)(2,1)} %refs_0_.1) | copy-start | bytes 2162692
  112.9 86.2 %copy-start.1 = (bf16[2,128,1408]{2,1,0:T(8,128)(2,1)S(1)}, bf16[2,128,1408]{2,1,0:T(8,128)(2,1)}, u32[]{:S(2)}) copy-start(bf16[2,128,1408]{2,1,0:T(8,128)(2,1)} %refs_1_.1) | copy-start | bytes 2162692
  112.9 86.2 %copy-start.2 = (bf16[2,352,512]{2,1,0:T(8,128)(2,1)S(1)}, bf16[2,352,512]{2,1,0:T(8,128)(2,1)}, u32[]{:S(2)}) copy-start(bf16[2,352,512]{2,1,0:T(8,128)(2,1)} %refs_2_.1) | copy-start | bytes 2162692
  113.0 86.2 %copy-start.3 = (f32[2,128,1408]{2,1,0:T(8,128)S(1)}, f32[2,128,1408]{2,1,0:T(8,128)}, u32[]{:S(2)}) copy-start(f32[2,128,1408]{2,1,0:T(8,128)} %refs_3_.1) | copy-start | bytes 4325380
  113.0 86.2 %copy-start.4 = (f32[2,128,1408]{2,1,0:T(8,128)S(1)}, f32[2,128,1408]{2,1,0:T(8,128)}, u32[]{:S(2)}) copy-start(f32[2,128,1408]{2,1,0:T(8,128)} %refs_4_.1) | copy-start | bytes 4325380
  113.0 86.2 %copy-start.5 = (f32[2,352,512]{2,1,0:T(8,128)S(1)}, f32[2,352,512]{2,1,0:T(8,128)}, u32[]{:S(2)}) copy-start(f32[2,352,512]{2,1,0:T(8,128)} %refs_5_.1) | copy-start | bytes 4325380
  113.0 86.2 %copy-start.6 = (f32[2,128,1408]{2,1,0:T(8,128)S(1)}, f32[2,128,1408]{2,1,0:T(8,128)}, u32[]{:S(2)}) copy-start(f32[2,128,1408]{2,1,0:T(8,128)} %refs_6_.1) | copy-start | bytes 4325380
  113.0 86.2 %copy-start.7 = (f32[2,128,1408]{2,1,0:T(8,128)S(1)}, f32[2,128,1408]{2,1,0:T(8,128)}, u32[]{:S(2)}) copy-start(f32[2,128,1408]{2,1,0:T(8,128)} %refs_7_.1) | copy-start | bytes 4325380
  113.0 86.2 %copy-start.8 = (f32[2,352,512]{2,1,0:T(8,128)S(1)}, f32[2,352,512]{2,1,0:T(8,128)}, u32[]{:S(2)}) copy-start(f32[2,352,512]{2,1,0:T(8,128)} %refs_8_.1) | copy-start | bytes 4325380

commit v3 on v2

--- a/solution.py
+++ b/solution.py
@@ -153,8 +153,12 @@
         acc_d[...] = jnp.zeros_like(acc_d)
         own(0, 0).wait_recv()
         from_x(0, 0)
+        from_x(0, 1)
         for p in range(4):
-            from_x(0, p + 1)
+            if p < 3:
+                from_x(0, p + 2)
+            else:
+                from_x(1, 0)
             from_y(0, p)
             arrived(0, p)
             first, units = CHUNKS[p]
@@ -172,6 +176,7 @@
                 up_and_gate(first, units, a_first[t], acts.at[t], t % 2)
                 gu_copy(p, t).start()
 
+        from_x(1, 1)
         from_y(0, 4)
         own(0, 1).wait_recv()
         arrived(0, 4)
@@ -179,11 +184,12 @@
 
         @pl.loop(0, 4)
         def _(t):
-            for p in range(4):
+            for p in range(2):
 
                 @pl.when(t == p)
                 def _():
-                    from_x(1, p)
+                    from_x(1, p + 2)
+                    from_y(1, p)
 
             down(x_ref[t], acts.at[t], t)
 
@@ -193,21 +199,13 @@
         def _(t):
             @pl.when(t == 0)
             def _():
-                from_y(1, 0)
-                from_y(1, 1)
-
-            @pl.when(t == 1)
-            def _():
                 from_x(1, 4)
-                from_y(1, 2)
-
-            @pl.when(t == 2)
-            def _():
-                from_y(1, 3)
-
-            @pl.when(t == 3)
-            def _():
-                from_y(1, 4)
+
+            for p in range(2, 5):
+
+                @pl.when(t == p - 1)
+                def _():
+                    from_y(1, p)
 
             x = x_ref[t]
             wide = x.astype(F32)

time: 206 us -> 204 us (level)
  Pallas kernels: 205 us -> 202 us
    pallas_call x1, Pallas kernels: 112 us -> 109 us  [step(): pl.pallas_call(first_kernel, grid=(2 + tiles,), in_specs=[pl.BlockSpec((t...]
where the time goes in v3:
time: 204 us; the launch traced here: 203 us
  Pallas kernels  202 us (99%)
    pallas_call x1, Pallas kernels, step(): pl.pallas_call(first_kernel, grid=(2 + tiles,), in_specs=[pl.BlockSpec((t...  109 us
    pallas_call x1, Pallas kernels, step(): pl.pallas_call(second_kernel, in_specs=[pl.BlockSpec(memory_space=pltpu.H...  86.9 us
    pallas_call x1, Pallas kernels, step(): pl.pallas_call(third_kernel, in_specs=[vmem] * (2 + len(arrays)), out_spe...  6.23 us

profile of v3, /device:TPU:0, one launch (start us, length us, event | category | flops | bytes accessed | tf_op | source)
XLA Modules:
  0.0 203.4 jit_solution(4556974544586418104)
XLA Ops:
  0.6 109.2 %gather_forward_and_last_layer.1 = (bf16[11,2,2,8,48,128]{5,4,3,2,1,0:T(8,128)(2,1)}, bf16[4,512,1024]{2,1,0:T(8,128)(2,1)}, f32[11,4,256,1024]{3,2,1,0:T(8,128)}, bf16[2,11,4,32,512]{4,3,2,1,0:T(8,128)(2,1)}) custom-call(bf16[8,512,512]{2,1,0:T(8,128)(2,1)} %bitcast.5, bf16[4096,512]{1,0:T(8,128)(2,1)} %bitcast.7, bf16[2,128,1408]{2,1,0:T(8,128)(2,1)} %refs_0_.1, ...), custom_call_target="tpu_custom_call" | custom-call | tf_op jit(solution)/shard_map/gather_forward_and_last_layer/pallas_call | solution.py:490
  109.9 0.0 copy-start
  109.9 0.0 copy-start.1
  109.9 0.0 copy-start.2
  109.9 0.0 copy-start.3
  109.9 0.0 copy-start.4
  109.9 0.0 copy-start.5
  110.0 0.0 copy-start.6
  110.0 0.0 copy-start.7
  110.0 0.0 copy-start.8
  110.0 86.9 %first_layer_and_sums.1 = (bf16[22,8,48,128]{3,2,1,0:T(8,128)(2,1)S(1)}, f32[8,128]{1,0:T(8,128)S(1)}) custom-call(bf16[4096,512]{1,0:T(8,128)(2,1)} %bitcast.6, bf16[4,512,1024]{2,1,0:T(8,128)(2,1)} %get-tuple-element.15.dh_any, f32[11,4,256,1024]{3,2,1,0:T(8,128)} %get-tuple-element.16.gu_any, bf16[2,11,4,32,512]{4,3,2,1,0:T(8,128)(2,1)} %get-tuple-element.17.wd_any, ...), custom_call_target="tpu_custom_call" | custom-call | tf_op jit(solution)/shard_map/first_layer_and_sums/pallas_call | solution.py:523
  196.9 0.0 copy-done
  196.9 0.0 copy-done.1
  196.9 0.0 copy-done.2
  196.9 0.0 copy-done.3
  196.9 0.0 copy-done.4
  197.0 0.0 copy-done.5
  197.0 0.0 copy-done.6
  197.0 0.0 copy-done.7
  197.0 0.0 copy-done.8
  197.0 6.2 %clip_and_adamw.1 = (bf16[2,128,1408]{2,1,0:T(8,128)(2,1)}, bf16[2,128,1408]{2,1,0:T(8,128)(2,1)}, bf16[2,352,512]{2,1,0:T(8,128)(2,1)}, f32[2,128,1408]{2,1,0:T...) custom-call(bf16[2,11,8,48,128]{4,3,2,1,0:T(8,128)(2,1)S(1)} %bitcas, ...), custom_call_target="tpu_custom_call" | custom-call | tf_op jit(solution)/shard_map/clip_and_adamw/pallas_call | solution.py:558
Async XLA Ops:
  109.9 87.0 %copy-start = (bf16[2,128,1408]{2,1,0:T(8,128)(2,1)S(1)}, bf16[2,128,1408]{2,1,0:T(8,128)(2,1)}, u32[]{:S(2)}) copy-start(bf16[2,128,1408]{2,1,0:T(8,128)(2,1)} %refs_0_.1) | copy-start | bytes 2162692
  109.9 87.0 %copy-start.1 = (bf16[2,128,1408]{2,1,0:T(8,128)(2,1)S(1)}, bf16[2,128,1408]{2,1,0:T(8,128)(2,1)}, u32[]{:S(2)}) copy-start(bf16[2,128,1408]{2,1,0:T(8,128)(2,1)} %refs_1_.1) | copy-start | bytes 2162692
  109.9 87.0 %copy-start.2 = (bf16[2,352,512]{2,1,0:T(8,128)(2,1)S(1)}, bf16[2,352,512]{2,1,0:T(8,128)(2,1)}, u32[]{:S(2)}) copy-start(bf16[2,352,512]{2,1,0:T(8,128)(2,1)} %refs_2_.1) | copy-start | bytes 2162692
  109.9 87.0 %copy-start.3 = (f32[2,128,1408]{2,1,0:T(8,128)S(1)}, f32[2,128,1408]{2,1,0:T(8,128)}, u32[]{:S(2)}) copy-start(f32[2,128,1408]{2,1,0:T(8,128)} %refs_3_.1) | copy-start | bytes 4325380
  109.9 87.0 %copy-start.4 = (f32[2,128,1408]{2,1,0:T(8,128)S(1)}, f32[2,128,1408]{2,1,0:T(8,128)}, u32[]{:S(2)}) copy-start(f32[2,128,1408]{2,1,0:T(8,128)} %refs_4_.1) | copy-start | bytes 4325380
  109.9 87.0 %copy-start.5 = (f32[2,352,512]{2,1,0:T(8,128)S(1)}, f32[2,352,512]{2,1,0:T(8,128)}, u32[]{:S(2)}) copy-start(f32[2,352,512]{2,1,0:T(8,128)} %refs_5_.1) | copy-start | bytes 4325380
  110.0 87.0 %copy-start.6 = (f32[2,128,1408]{2,1,0:T(8,128)S(1)}, f32[2,128,1408]{2,1,0:T(8,128)}, u32[]{:S(2)}) copy-start(f32[2,128,1408]{2,1,0:T(8,128)} %refs_6_.1) | copy-start | bytes 4325380
  110.0 87.0 %copy-start.7 = (f32[2,128,1408]{2,1,0:T(8,128)S(1)}, f32[2,128,1408]{2,1,0:T(8,128)}, u32[]{:S(2)}) copy-start(f32[2,128,1408]{2,1,0:T(8,128)} %refs_7_.1) | copy-start | bytes 4325380
  110.0 87.0 %copy-start.8 = (f32[2,352,512]{2,1,0:T(8,128)S(1)}, f32[2,352,512]{2,1,0:T(8,128)}, u32[]{:S(2)}) copy-start(f32[2,352,512]{2,1,0:T(8,128)} %refs_8_.1) | copy-start | bytes 4325380

commit v4 on v3

--- a/solution.py
+++ b/solution.py
@@ -71,8 +71,8 @@
 
 
 def first_kernel(
-    x_ref, dy_ref, gate_ref, up_ref, down_ref, u_ref, dh_ref, gu_out, wd_out,
-    wgu, wd, h1s, acts, a_first, stage, dgu, wdt, acc_gu, acc_d, own_send, own_recv, send, recv, gu_sem, out_sem,
+    x_ref, dy_ref, gate_ref, up_ref, down_ref, u_out, dh_ref, gu_out, wd_out,
+    u, wgu, wd, h1s, acts, a_first, stage, dgu, wdt, acc_gu, acc_d, own_send, own_recv, send, recv, gu_sem, u_sem, out_sem,
 ):
     i = pl.program_id(0)
     x, c, y, z = place()
@@ -98,6 +98,9 @@
         return remote(ref, ref, own_send.at[l, k], own_recv.at[l, k], to_core)
 
     wd_copy = pltpu.make_async_copy(wd, wd_out, out_sem.at[0])
+
+    def u_copy(n):
+        return pltpu.make_async_copy(u.at[n], u_out.at[n], u_sem.at[n])
 
     def gu_copy(p, t):
         first, units = CHUNKS[p]
@@ -248,9 +251,12 @@
     def _():
         @pl.loop(0, UNITS)
         def _(n):
-            pack(n, acc_gu, acc_d, n, u_ref)
+            pack(n, acc_gu, acc_d, n, u)
+            u_copy(n).start()
 
         wd_copy.wait()
+        for n in range(UNITS):
+            u_copy(n).wait()
         for p in range(4):
             for t in (6, 7):
                 gu_copy(p, t).wait()
@@ -288,7 +294,7 @@
         rows = pl.ds(WIDE * t, WIDE)
         return pltpu.make_async_copy(x_any.at[rows], a0.at[t], tile_sem.at[t, 0]), pltpu.make_async_copy(dh_any.at[t], dh.at[t], tile_sem.at[t, 1])
 
-    for one in (own_load(0), own_load(1), wd_load, gu_load(0, 0), *tile_loads(0)):
+    for one in (own_load(0), gu_load(0, 0), wd_load, *tile_loads(0), own_load(1)):
         one.start()
     for t in range(1, 4):
         for one in tile_loads(t):
@@ -374,7 +380,6 @@
     own_load(0).wait()
     greeted()
     tick(0)
-    own_load(1).wait()
     wd_load.wait()
     for number, (first, units) in enumerate(CHUNKS):
         acc_d[...] = jnp.zeros_like(acc_d)
@@ -408,6 +413,12 @@
             acc_d[: LANE * units, :] += nt(act[: LANE * units, :], h)
             acc_gu[: PAIR * units, :] += nn(dgu[: PAIR * units, :], a)
 
+            if number == 0:
+
+                @pl.when(t == 0)
+                def _():
+                    own_load(1).wait()
+
             tick(5 * number + t + 1)
 
         @pl.loop(0, units)
@@ -495,7 +506,7 @@
             pl.BlockSpec((TT, D), lambda i: (jnp.maximum(i - 2, 0), 0)),
             once(w_gate.shape), once(w_up.shape), once(w_down.shape),
         ],
-        out_specs=[once(unit), pl.BlockSpec((1, D, TT), lambda i: (jnp.maximum(i - 2, 0) // 2, 0, jnp.maximum(i - 2, 0) % 2)), any_, any_],
+        out_specs=[any_, pl.BlockSpec((1, D, TT), lambda i: (jnp.maximum(i - 2, 0) // 2, 0, jnp.maximum(i - 2, 0) % 2)), any_, any_],
         out_shape=[
             jax.ShapeDtypeStruct(unit, BF),
             jax.ShapeDtypeStruct((tiles // 2, D, WIDE), BF),
@@ -503,6 +514,7 @@
             jax.ShapeDtypeStruct((2, UNITS, 4, SEG, D), BF),
         ],
         scratch_shapes=[
+            pltpu.VMEM(unit, BF),
             pltpu.VMEM((2, UNITS, 2, LANE, D), BF),
             pltpu.VMEM((2, UNITS, 4, SEG, D), BF),
             pltpu.VMEM((tiles, D, TT), BF),
@@ -513,7 +525,7 @@
             pltpu.VMEM((D, FF), BF),
             pltpu.VMEM((2 * FF, D), F32),
             pltpu.VMEM((FF, D), F32),
-            dma((2, 2)), dma((2, 2)), dma((2, 5, 4)), dma((2, 5, 4)), dma((4, 2)), dma((1,)),
+            dma((2, 2)), dma((2, 2)), dma((2, 5, 4)), dma((2, 5, 4)), dma((4, 2)), dma((UNITS,)), dma((1,)),
         ],
         compiler_params=pltpu.CompilerParams(vmem_limit_bytes=VMEM_LIMIT, collective_id=0, has_side_effects=True),
         name="gather_forward_and_last_layer",

time: 204 us -> 203 us (level)
  no operation moved by 1% of the time
where the time goes in v4:
time: 203 us; the launch traced here: 202 us
  Pallas kernels  201 us (99%)
    pallas_call x1, Pallas kernels, step(): pl.pallas_call(first_kernel, grid=(2 + tiles,), in_specs=[pl.BlockSpec((t...  109 us
    pallas_call x1, Pallas kernels, step(): pl.pallas_call(second_kernel, in_specs=[pl.BlockSpec(memory_space=pltpu.H...  85.7 us
    pallas_call x1, Pallas kernels, step(): pl.pallas_call(third_kernel, in_specs=[vmem] * (2 + len(arrays)), out_spe...  6.23 us

profile of v4, /device:TPU:0, one launch (start us, length us, event | category | flops | bytes accessed | tf_op | source)
XLA Modules:
  0.0 202.4 jit_solution(16463461403534543434)
XLA Ops:
  0.6 109.5 %gather_forward_and_last_layer.1 = (bf16[11,2,2,8,48,128]{5,4,3,2,1,0:T(8,128)(2,1)}, bf16[4,512,1024]{2,1,0:T(8,128)(2,1)}, f32[11,4,256,1024]{3,2,1,0:T(8,128)}, bf16[2,11,4,32,512]{4,3,2,1,0:T(8,128)(2,1)}) custom-call(bf16[8,512,512]{2,1,0:T(8,128)(2,1)} %bitcast.5, bf16[4096,512]{1,0:T(8,128)(2,1)} %bitcast.7, bf16[2,128,1408]{2,1,0:T(8,128)(2,1)} %refs_0_.1, ...), custom_call_target="tpu_custom_call" | custom-call | tf_op jit(solution)/shard_map/gather_forward_and_last_layer/pallas_call | solution.py:501
  110.1 0.0 copy-start
  110.1 0.0 copy-start.1
  110.2 0.0 copy-start.2
  110.2 0.0 copy-start.3
  110.2 0.0 copy-start.4
  110.2 0.0 copy-start.5
  110.2 0.0 copy-start.6
  110.2 0.0 copy-start.7
  110.2 0.0 copy-start.8
  110.2 85.7 %first_layer_and_sums.1 = (bf16[22,8,48,128]{3,2,1,0:T(8,128)(2,1)S(1)}, f32[8,128]{1,0:T(8,128)S(1)}) custom-call(bf16[4096,512]{1,0:T(8,128)(2,1)} %bitcast.6, bf16[4,512,1024]{2,1,0:T(8,128)(2,1)} %get-tuple-element.15.dh_any, f32[11,4,256,1024]{3,2,1,0:T(8,128)} %get-tuple-element.16.gu_any, bf16[2,11,4,32,512]{4,3,2,1,0:T(8,128)(2,1)} %get-tuple-element.17.wd_any, ...), custom_call_target="tpu_custom_call" | custom-call | tf_op jit(solution)/shard_map/first_layer_and_sums/pallas_call | solution.py:535
  195.9 0.0 copy-done
  195.9 0.0 copy-done.1
  195.9 0.0 copy-done.2
  196.0 0.0 copy-done.3
  196.0 0.0 copy-done.4
  196.0 0.0 copy-done.5
  196.0 0.0 copy-done.6
  196.0 0.0 copy-done.7
  196.0 0.0 copy-done.8
  196.0 6.2 %clip_and_adamw.1 = (bf16[2,128,1408]{2,1,0:T(8,128)(2,1)}, bf16[2,128,1408]{2,1,0:T(8,128)(2,1)}, bf16[2,352,512]{2,1,0:T(8,128)(2,1)}, f32[2,128,1408]{2,1,0:T...) custom-call(bf16[2,11,8,48,128]{4,3,2,1,0:T(8,128)(2,1)S(1)} %bitcas, ...), custom_call_target="tpu_custom_call" | custom-call | tf_op jit(solution)/shard_map/clip_and_adamw/pallas_call | solution.py:570
Async XLA Ops:
  110.1 85.8 %copy-start = (bf16[2,128,1408]{2,1,0:T(8,128)(2,1)S(1)}, bf16[2,128,1408]{2,1,0:T(8,128)(2,1)}, u32[]{:S(2)}) copy-start(bf16[2,128,1408]{2,1,0:T(8,128)(2,1)} %refs_0_.1) | copy-start | bytes 2162692
  110.1 85.8 %copy-start.1 = (bf16[2,128,1408]{2,1,0:T(8,128)(2,1)S(1)}, bf16[2,128,1408]{2,1,0:T(8,128)(2,1)}, u32[]{:S(2)}) copy-start(bf16[2,128,1408]{2,1,0:T(8,128)(2,1)} %refs_1_.1) | copy-start | bytes 2162692
  110.2 85.8 %copy-start.2 = (bf16[2,352,512]{2,1,0:T(8,128)(2,1)S(1)}, bf16[2,352,512]{2,1,0:T(8,128)(2,1)}, u32[]{:S(2)}) copy-start(bf16[2,352,512]{2,1,0:T(8,128)(2,1)} %refs_2_.1) | copy-start | bytes 2162692
  110.2 85.8 %copy-start.3 = (f32[2,128,1408]{2,1,0:T(8,128)S(1)}, f32[2,128,1408]{2,1,0:T(8,128)}, u32[]{:S(2)}) copy-start(f32[2,128,1408]{2,1,0:T(8,128)} %refs_3_.1) | copy-start | bytes 4325380
  110.2 85.8 %copy-start.4 = (f32[2,128,1408]{2,1,0:T(8,128)S(1)}, f32[2,128,1408]{2,1,0:T(8,128)}, u32[]{:S(2)}) copy-start(f32[2,128,1408]{2,1,0:T(8,128)} %refs_4_.1) | copy-start | bytes 4325380
  110.2 85.8 %copy-start.5 = (f32[2,352,512]{2,1,0:T(8,128)S(1)}, f32[2,352,512]{2,1,0:T(8,128)}, u32[]{:S(2)}) copy-start(f32[2,352,512]{2,1,0:T(8,128)} %refs_5_.1) | copy-start | bytes 4325380
  110.2 85.8 %copy-start.6 = (f32[2,128,1408]{2,1,0:T(8,128)S(1)}, f32[2,128,1408]{2,1,0:T(8,128)}, u32[]{:S(2)}) copy-start(f32[2,128,1408]{2,1,0:T(8,128)} %refs_6_.1) | copy-start | bytes 4325380
  110.2 85.8 %copy-start.7 = (f32[2,128,1408]{2,1,0:T(8,128)S(1)}, f32[2,128,1408]{2,1,0:T(8,128)}, u32[]{:S(2)}) copy-start(f32[2,128,1408]{2,1,0:T(8,128)} %refs_7_.1) | copy-start | bytes 4325380
  110.2 85.8 %copy-start.8 = (f32[2,352,512]{2,1,0:T(8,128)S(1)}, f32[2,352,512]{2,1,0:T(8,128)}, u32[]{:S(2)}) copy-start(f32[2,352,512]{2,1,0:T(8,128)} %refs_8_.1) | copy-start | bytes 4325380
